TPU v7x, 256 devices: a whole 4x4x8 slice. The times are simulated.
256 devices in a mesh: dp: 128 (over y, x, z), mp: 2 (over core).
Axes of the slice: x: 4, y: 4, z: 8, core: 2. Of those that a mesh axis runs over, the one named last changes fastest.
Arguments:
- media: bfloat16 [2048, 256, 1024], P('dp'), may hold values from -6 to 6
- slot_clip: int32 [2048], P('dp'), may hold values from 0 to 127, as said below
- time_table: bfloat16 [144, 1024], replicated, may hold values from -6 to 6
- latents_init: float32 [64, 1024], replicated, may hold values from -6 to 6
- media_gain: float32 [2, 1024], replicated, may hold values from 0.5 to 1.5
- latent_gain: float32 [2, 1024], replicated, may hold values from 0.5 to 1.5
- final_gain: float32 [1024], replicated, may hold values from 0.5 to 1.5
- w_query: bfloat16 [2, 1024, 512], P(None, None, 'mp'), may hold values from -24 to 24
- w_key: bfloat16 [2, 1024, 512], P(None, None, 'mp'), may hold values from -0.1875 to 0.1875
- w_value: bfloat16 [2, 1024, 512], P(None, None, 'mp'), may hold values from -0.1875 to 0.1875
- w_out: bfloat16 [2, 512, 1024], P(None, 'mp'), may hold values from -0.5 to 0.5
Outputs:
- resampled: float32 [128, 64, 1024], P('dp')
Inputs may be any that keep to these rules, and one draw needn't show every extreme that they name: `slot_clip`: slot b lies on dp index b // 16, and its clip differs from that index by at most 4; differences of +4 and -4 both occur in every draw.
All inputs are finite; a program needn't handle non-finite values.
Results may differ from a plain program's by a relative error of at most 0.0085.
The roundings to bfloat16 on the way count: a program that leaves them out, or rounds other values in their place, can miss the bound.
Values may be sent and summed in bfloat16 or wider, within the bound.
A program may use at most 128 MiB of HBM per device.

v0:
```python
import jax
import jax.numpy as jnp
from jax import lax
from jax.sharding import Mesh
from jax.sharding import PartitionSpec as P

HEAD_DIM = 64
LAYERS = 2
REACH = 4
DP = ("dp_0", "dp_1", "dp_2")


epsilon = 1e-05
floor_score = -1e30


def neutral_like(x, identity):
    return jnp.zeros_like(x) + jnp.asarray(identity, x.dtype)


def entering(x, axes, combine, identity):
    before = start = neutral_like(x, identity)
    running = x
    for axis in reversed(axes):
        count, index = (lax.axis_size(axis), lax.axis_index(axis))
        pieces = lax.all_gather(running, axis)
        inside, running = (start, start)
        for k in range(count):
            passed = k < index
            running = combine(running, pieces[k])
            inside = jnp.where(passed, running, inside)
        before = combine(inside, before)
    return before


def passed_along(value, axis, steps):
    count = lax.axis_size(axis)
    initial, last = (max(0, -steps), min(count, count - steps))
    return lax.ppermute(value, axis, [(source, source + steps) for source in range(initial, last)])


def copy_for_each(x, axis):
    copies = jnp.broadcast_to(x, (lax.axis_size(axis), *x.shape))
    return lax.all_to_all(copies, axis, split_axis=0, concat_axis=0, tiled=True)


def over_copies(x, axis):
    return copy_for_each(x, axis).astype(jnp.float32).sum(axis=0)


def normalize(values):
    mean = jnp.mean(values, axis=-1, keepdims=True)
    center = values - mean
    spread = jnp.mean(center * center, axis=-1, keepdims=True)
    return center / jnp.sqrt(spread + epsilon)


def weigh_acc(acc, weight):
    heads = weight.shape[-2]
    shaped = acc.reshape(acc.shape[:-1] + (heads, acc.shape[-1] // heads))
    scaled = shaped * jnp.swapaxes(weight, -1, -2)[..., None]
    return scaled.reshape(acc.shape)


def divide_heads(acc, total):
    heads = total.shape[-2]
    shaped = acc.reshape(acc.shape[:-1] + (heads, acc.shape[-1] // heads))
    scaled = shaped / jnp.swapaxes(total, -1, -2)[..., None]
    return scaled.reshape(acc.shape)


def block_stats(queries, keys, values):
    scores = jnp.einsum("bqhd,bkhd->bhqk", queries, keys, preferred_element_type=jnp.float32)
    top = jnp.max(scores, axis=-1)
    expo = jnp.exp(scores - top[..., None])
    total = jnp.sum(expo, axis=-1)
    weights = expo.astype(jnp.bfloat16)
    acc = jnp.einsum("bhqk,bkhd->bqhd", weights, values, preferred_element_type=jnp.float32)
    return (top, total, acc.reshape(acc.shape[0], acc.shape[1], -1))


def merge_pair(first, second):
    top_first = jnp.where(first[1] > 0.5, first[0], floor_score)
    top_second = jnp.where(second[1] > 0.5, second[0], floor_score)
    top = jnp.maximum(top_first, top_second)
    weight_first = jnp.exp(top_first - top)
    weight_second = jnp.exp(top_second - top)
    total = weight_first * first[1] + weight_second * second[1]
    acc = weigh_acc(first[2], weight_first) + weigh_acc(second[2], weight_second)
    return (top, total, acc)


def add_counts(earlier, later):
    return earlier + later


def local(
    media,
    slot_clip,
    time_table,
    latents_init,
    media_gain,
    latent_gain,
    final_gain,
    w_query,
    w_key,
    w_value,
    w_out,
):
    frames, patches, width = media.shape
    inner = w_query.shape[2]
    heads = inner // HEAD_DIM
    latent_count = latents_init.shape[0]
    span = 2 * REACH + 1
    here = lax.axis_index(DP)
    offsets = slot_clip - here + REACH
    same = slot_clip[:, None] == slot_clip[None, :]
    lower = jnp.arange(frames)[None, :] < jnp.arange(frames)[:, None]
    within = jnp.sum((same & lower).astype(jnp.int32), axis=1)
    clips = lax.axis_size(DP)
    member_clip = slot_clip[:, None] == jnp.arange(clips)[None, :]
    tally = jnp.sum(member_clip.astype(jnp.int32), axis=0)
    before = entering(tally, DP, add_counts, jnp.zeros_like(tally))
    earlier = jnp.sum(jnp.where(member_clip, before[None, :], 0), axis=1)
    frame_index = earlier + within
    table_rows = time_table.shape[0]
    picker = (frame_index[:, None] == jnp.arange(table_rows)[None, :]).astype(jnp.bfloat16)
    stamp = jnp.dot(picker, time_table, preferred_element_type=jnp.float32)
    unit = normalize(media.astype(jnp.float32) + stamp[:, None, :])
    member = offsets[:, None] == jnp.arange(span)[None, :]
    share = member.astype(jnp.float32)
    state = latents_init
    for layer in range(LAYERS):
        normed = (unit * media_gain[layer]).astype(jnp.bfloat16).reshape(frames * patches, width)
        keys = jnp.dot(normed, w_key[layer], preferred_element_type=jnp.float32).astype(
            jnp.bfloat16
        )
        vals = jnp.dot(normed, w_value[layer], preferred_element_type=jnp.float32).astype(
            jnp.bfloat16
        )
        keys, vals = (
            keys.reshape(frames, patches, heads, HEAD_DIM),
            vals.reshape(frames, patches, heads, HEAD_DIM),
        )
        lat_norm = (normalize(state) * latent_gain[layer]).astype(jnp.bfloat16)
        query = (
            jnp.dot(lat_norm, w_query[layer], preferred_element_type=jnp.float32)
            * HEAD_DIM ** (-0.5)
        ).astype(jnp.bfloat16)
        self_keys = jnp.dot(lat_norm, w_key[layer], preferred_element_type=jnp.float32).astype(
            jnp.bfloat16
        )
        self_vals = jnp.dot(lat_norm, w_value[layer], preferred_element_type=jnp.float32).astype(
            jnp.bfloat16
        )
        window = query[None]
        length = 1
        while length < REACH + 1:
            needed = min(2 * length, REACH + 1)
            extra = needed - length
            received = passed_along(window[length - extra :], DP, length)
            window = jnp.concatenate([received, window], axis=0)
            length = needed
        upward = query[None]
        length = 1
        while length < REACH + 1:
            needed = min(2 * length, REACH + 1)
            extra = needed - length
            arrived_up = passed_along(upward[:extra], DP, -length)
            upward = jnp.concatenate([upward, arrived_up], axis=0)
            length = needed
        near_queries = jnp.concatenate([window, upward[1:]], axis=0)
        chosen = jnp.take(near_queries, offsets, axis=0).reshape(
            frames, latent_count, heads, HEAD_DIM
        )
        top, total, acc = block_stats(chosen, keys, vals)
        part_top = jnp.max(jnp.where(member[:, :, None, None], top[:, None], floor_score), axis=0)
        weight = jnp.exp(top - jnp.take(part_top, offsets, axis=0))
        part_total = jnp.sum(share[:, :, None, None] * (weight * total)[:, None], axis=0)
        part_acc = jnp.sum(share[:, :, None, None] * weigh_acc(acc, weight)[:, None], axis=0)
        shaped = (1, latent_count, heads, HEAD_DIM)
        own_top, own_total, own_acc = block_stats(
            query.reshape(shaped), self_keys.reshape(shaped), self_vals.reshape(shaped)
        )
        own = (own_top[0], own_total[0], own_acc[0])
        merged = own
        for slot in range(span):
            piece = (part_top[slot], part_total[slot], part_acc[slot])
            if slot != REACH:
                piece = passed_along((piece[0], piece[1], piece[2]), DP, slot - REACH)
            merged = merge_pair(merged, piece)
        attn = divide_heads(merged[2], merged[1]).astype(jnp.bfloat16)
        change = jnp.dot(attn, w_out[layer], preferred_element_type=jnp.float32)
        state = state + over_copies(change.astype(jnp.bfloat16), "mp").astype(jnp.float32)
    result = normalize(state) * final_gain
    return result[None]


def solution(mesh):
    finer = Mesh(mesh.devices.reshape(4, 4, 8, mesh.shape["mp"]), ("dp_0", "dp_1", "dp_2", "mp"))
    return jax.shard_map(
        local,
        mesh=finer,
        in_specs=(
            P(DP, None, None),
            P(DP),
            P(),
            P(),
            P(),
            P(),
            P(),
            P(None, None, "mp"),
            P(None, None, "mp"),
            P(None, None, "mp"),
            P(None, "mp", None),
        ),
        out_specs=P(DP, None, None),
        check_vma=False,
    )
```

profile of v0, /device:TPU:25, one launch (start us, length us, event | category | flops | bytes accessed | tf_op | source)
XLA Modules:
  0.0 456.9 jit_solution(3464703920988075584)
XLA Ops:
  4.5 9.9 %collective-permute-start.3 = (bf16[1,64,256]{2,1,0:T(8,128)(2,1)S(1)}, bf16[1,64,256]{2,1,0:T(8,128)(2,1)S(1)}, u32[]{:S(2)}, u32[]{:S(2)}) collective-permute-start(bf16[1,64,256]{2,1,0:T(8,128)(2,1)S(1)} %bitcast.400), channel_id=1, source_target_pairs={{2,0},{4,2},{6,4},{8,6},{10,8},{12,10},{14,12},{16,14},{18,16},{20... | collective-permute-start | bytes 98312 | tf_op jit(solution)/shard_map/ppermute | solution.py:39
  28.6 11.0 %all-gather.1 = s32[8,1,128]{2,1,0:T(1,128)S(1)} all-gather(s32[1,1,128]{2,1,0:T(1,128)S(1)} %bitcast.421), channel_id=2, replica_groups=mesh['dp_0'=4,'dp_1'=4,'dp_2'=8,'mp'=2] {'dp_2'}, dimensions={0}, use_global_device_ids=true | all-gather | bytes 4608 | tf_op jit(solution)/shard_map/all_gather | solution.py:26
  39.6 6.4 %all-gather.2 = s32[4,1,128]{2,1,0:T(1,128)S(1)} all-gather(s32[1,1,128]{2,1,0:T(1,128)S(1)} %bitcast.414), channel_id=1, replica_groups=mesh['dp_0'=4,'dp_1'=4,'dp_2'=8,'mp'=2] {'dp_1'}, dimensions={0}, use_global_device_ids=true | all-gather | bytes 2560 | tf_op jit(solution)/shard_map/all_gather | solution.py:26
  46.1 7.8 %all-gather.3 = s32[4,1,128]{2,1,0:T(1,128)S(1)} all-gather(s32[1,1,128]{2,1,0:T(1,128)S(1)} %slice_add_fusion.3), channel_id=1, replica_groups=mesh['dp_0'=4,'dp_1'=4,'dp_2'=8,'mp'=2] {'dp_0'}, dimensions={0}, use_global_device_ids=true | all-gather | bytes 2560 | tf_op jit(solution)/shard_map/all_gather | solution.py:26
  67.5 10.6 %multiply_convert_fusion = (bf16[16,256,1024]{2,1,0:T(8,128)(2,1)S(1)}, bf16[16,256,1024]{2,1,0:T(8,128)(2,1)S(1)}) fusion(bf16[16,256,1024]{2,1,0:T(8,128)(2,1)S(1)} %copy-done.2, f32[1024]{0:T(1024)S(1)} %bitcast.412, f32[16,256]{1,0:T(8,128)S(1)} %add_sqrt_fusion, f32[16,256]{1,0:T(8,128)S(1)} %broadcast_multiply_fusion, f32[16,1024]{1,0:T(8,128)S(1)} %fusion.99, ...), kind=kLoop, calls=%fused_computation.4 | loop fusion | flops 33554432 | bytes 25272320 | tf_op jit(solution)/shard_map/convert_element_type | solution.py:134
  92.7 7.1 %reshape.490 = bf16[16,256,4,64]{3,2,1,0:T(4,128)(2,1)} reshape(bf16[4096,256]{1,0:T(8,128)(2,1)} %convolution_convert_fusion.3) | data formatting | bytes 4194304 | tf_op jit(solution)/shard_map/reshape | solution.py:142
  103.1 7.4 %reshape.492 = bf16[16,256,4,64]{3,2,1,0:T(4,128)(2,1)} reshape(bf16[4096,256]{1,0:T(8,128)(2,1)} %convolution_convert_fusion.1) | data formatting | bytes 4194304 | tf_op jit(solution)/shard_map/reshape | solution.py:142
  120.0 5.8 %collective-permute-done.2 = bf16[2,64,256]{2,1,0:T(8,128)(2,1)S(1)} collective-permute-done((bf16[2,64,256]{2,1,0:T(8,128)(2,1)S(1)}, bf16[2,64,256]{2,1,0:T(8,128)(2,1)S(1)}, u32[]{:S(2)}, u32[]{:S(2)}) %collective-permute-start.2) | collective-permute-done | bytes 65568 | tf_op jit(solution)/shard_map/ppermute | solution.py:39
  138.7 7.3 %collective-permute-start.28 = (f32[4,64]{1,0:T(4,128)S(1)}, f32[4,64]{1,0:T(4,128)S(1)}, u32[]{:S(2)}, u32[]{:S(2)}) collective-permute-start(f32[4,64]{1,0:T(4,128)S(1)} %get-tuple-element.96), channel_id=1, source_target_pairs={{0,8},{2,10},{4,12},{6,14},{8,16},{10,18},{12,20},{14,22},{16,24},... | collective-permute-start | bytes 3080 | tf_op jit(solution)/shard_map/ppermute | solution.py:39
  171.6 6.4 %collective-permute-start.13 = (f32[4,64]{1,0:T(4,128)S(1)}, f32[4,64]{1,0:T(4,128)S(1)}, u32[]{:S(2)}, u32[]{:S(2)}) collective-permute-start(f32[4,64]{1,0:T(4,128)S(1)} %get-tuple-element.101), channel_id=1, source_target_pairs={{4,0},{6,2},{8,4},{10,6},{12,8},{14,10},{16,12},{18,14},{20,16},{2... | collective-permute-start | bytes 3080 | tf_op jit(solution)/shard_map/ppermute | solution.py:39
  180.5 7.0 %collective-permute-start.16 = (f32[4,64]{1,0:T(4,128)S(1)}, f32[4,64]{1,0:T(4,128)S(1)}, u32[]{:S(2)}, u32[]{:S(2)}) collective-permute-start(f32[4,64]{1,0:T(4,128)S(1)} %get-tuple-element.100), channel_id=1, source_target_pairs={{2,0},{4,2},{6,4},{8,6},{10,8},{12,10},{14,12},{16,14},{18,16},{20... | collective-permute-start | bytes 3080 | tf_op jit(solution)/shard_map/ppermute | solution.py:39
  210.8 6.1 %collective-permute-start.8 = (f32[64,256]{1,0:T(8,128)S(1)}, f32[64,256]{1,0:T(8,128)S(1)}, u32[]{:S(2)}, u32[]{:S(2)}) collective-permute-start(f32[64,256]{1,0:T(8,128)S(1)} %get-tuple-element.63), channel_id=1, source_target_pairs={{8,0},{10,2},{12,4},{14,6},{16,8},{18,10},{20,12},{22,14},{24,16},... | collective-permute-start | bytes 196616 | tf_op jit(solution)/shard_map/ppermute | solution.py:39
  226.2 7.3 %collective-permute-start.17 = (f32[64,256]{1,0:T(8,128)}, f32[64,256]{1,0:T(8,128)}, u32[]{:S(2)}, u32[]{:S(2)}) collective-permute-start(f32[64,256]{1,0:T(8,128)} %get-tuple-element.68), channel_id=1, source_target_pairs={{2,0},{4,2},{6,4},{8,6},{10,8},{12,10},{14,12},{16,14},{18,16},{20... | collective-permute-start | bytes 196616 | tf_op jit(solution)/shard_map/ppermute | solution.py:39
  237.8 6.6 %collective-permute-start.11 = (f32[64,256]{1,0:T(8,128)S(1)}, f32[64,256]{1,0:T(8,128)}, u32[]{:S(2)}, u32[]{:S(2)}) collective-permute-start(f32[64,256]{1,0:T(8,128)S(1)} %get-tuple-element.70), channel_id=1, source_target_pairs={{6,0},{8,2},{10,4},{12,6},{14,8},{16,10},{18,12},{20,14},{22,16},{... | collective-permute-start | bytes 196616 | tf_op jit(solution)/shard_map/ppermute | solution.py:39
  253.2 22.2 %all_to_all.10 = bf16[2,64,1024]{2,1,0:T(8,128)(2,1)S(1)} all-to-all(bf16[2,64,1024]{2,1,0:T(8,128)(2,1)S(1)} %broadcast_in_dim.204), channel_id=1, replica_groups=mesh['dp_0'=4,'dp_1'=4,'dp_2'=8,'mp'=2] {'mp'}, dimensions={0} | all-to-all | bytes 524288 | tf_op jit(solution)/shard_map/all_to_all | solution.py:44
  278.8 7.3 %collective-permute-start.35 = (bf16[1,64,256]{2,1,0:T(8,128)(2,1)S(1)}, bf16[1,64,256]{2,1,0:T(8,128)(2,1)S(1)}, u32[]{:S(2)}, u32[]{:S(2)}) collective-permute-start(bf16[1,64,256]{2,1,0:T(8,128)(2,1)S(1)} %bitcast.406), channel_id=1, source_target_pairs={{8,0},{10,2},{12,4},{14,6},{16,8},{18,10},{20,12},{22,14},{24,16},... | collective-permute-start | bytes 98312 | tf_op jit(solution)/shard_map/ppermute | solution.py:39
  301.9 8.2 %collective-permute-done.32 = bf16[2,64,256]{2,1,0:T(8,128)(2,1)S(1)} collective-permute-done((bf16[2,64,256]{2,1,0:T(8,128)(2,1)S(1)}, bf16[2,64,256]{2,1,0:T(8,128)(2,1)S(1)}, u32[]{:S(2)}, u32[]{:S(2)}) %collective-permute-start.32) | collective-permute-done | bytes 65568 | tf_op jit(solution)/shard_map/ppermute | solution.py:39
  323.1 7.2 %collective-permute-start.58 = (f32[4,64]{1,0:T(4,128)S(1)}, f32[4,64]{1,0:T(4,128)S(1)}, u32[]{:S(2)}, u32[]{:S(2)}) collective-permute-start(f32[4,64]{1,0:T(4,128)S(1)} %get-tuple-element.80), channel_id=1, source_target_pairs={{0,8},{2,10},{4,12},{6,14},{8,16},{10,18},{12,20},{14,22},{16,24},... | collective-permute-start | bytes 3080 | tf_op jit(solution)/shard_map/ppermute | solution.py:39
  330.3 5.8 %collective-permute-start.40 = (f32[4,64]{1,0:T(4,128)S(1)}, f32[4,64]{1,0:T(4,128)S(1)}, u32[]{:S(2)}, u32[]{:S(2)}) collective-permute-start(f32[4,64]{1,0:T(4,128)S(1)} %get-tuple-element.86), channel_id=1, source_target_pairs={{6,0},{8,2},{10,4},{12,6},{14,8},{16,10},{18,12},{20,14},{22,16},{... | collective-permute-start | bytes 3080 | tf_op jit(solution)/shard_map/ppermute | solution.py:39
  355.5 6.4 %collective-permute-start.43 = (f32[4,64]{1,0:T(4,128)S(1)}, f32[4,64]{1,0:T(4,128)S(1)}, u32[]{:S(2)}, u32[]{:S(2)}) collective-permute-start(f32[4,64]{1,0:T(4,128)S(1)} %get-tuple-element.85), channel_id=1, source_target_pairs={{4,0},{6,2},{8,4},{10,6},{12,8},{14,10},{16,12},{18,14},{20,16},{2... | collective-permute-start | bytes 3080 | tf_op jit(solution)/shard_map/ppermute | solution.py:39
  363.9 8.7 %collective-permute-start.46 = (f32[4,64]{1,0:T(4,128)S(1)}, f32[4,64]{1,0:T(4,128)S(1)}, u32[]{:S(2)}, u32[]{:S(2)}) collective-permute-start(f32[4,64]{1,0:T(4,128)S(1)} %get-tuple-element.84), channel_id=1, source_target_pairs={{2,0},{4,2},{6,4},{8,6},{10,8},{12,10},{14,12},{16,14},{18,16},{20... | collective-permute-start | bytes 3080 | tf_op jit(solution)/shard_map/ppermute | solution.py:39
  411.3 7.3 %collective-permute-start.47 = (f32[64,256]{1,0:T(8,128)}, f32[64,256]{1,0:T(8,128)}, u32[]{:S(2)}, u32[]{:S(2)}) collective-permute-start(f32[64,256]{1,0:T(8,128)} %get-tuple-element.60), channel_id=1, source_target_pairs={{2,0},{4,2},{6,4},{8,6},{10,8},{12,10},{14,12},{16,14},{18,16},{20... | collective-permute-start | bytes 196616 | tf_op jit(solution)/shard_map/ppermute | solution.py:39
  422.9 6.7 %collective-permute-start.41 = (f32[64,256]{1,0:T(8,128)}, f32[64,256]{1,0:T(8,128)}, u32[]{:S(2)}, u32[]{:S(2)}) collective-permute-start(f32[64,256]{1,0:T(8,128)} %get-tuple-element.62), channel_id=1, source_target_pairs={{6,0},{8,2},{10,4},{12,6},{14,8},{16,10},{18,12},{20,14},{22,16},{... | collective-permute-start | bytes 196616 | tf_op jit(solution)/shard_map/ppermute | solution.py:39
  440.8 14.4 %all_to_all.11 = bf16[2,64,1024]{2,1,0:T(8,128)(2,1)S(1)} all-to-all(bf16[2,64,1024]{2,1,0:T(8,128)(2,1)S(1)} %broadcast_in_dim.207), channel_id=1, replica_groups=mesh['dp_0'=4,'dp_1'=4,'dp_2'=8,'mp'=2] {'mp'}, dimensions={0} | all-to-all | bytes 524288 | tf_op jit(solution)/shard_map/all_to_all | solution.py:44
  (395 shorter events, 253.4 us)
Async XLA Ops:
  4.5 109.3 %collective-permute-start.3 = (bf16[1,64,256]{2,1,0:T(8,128)(2,1)S(1)}, bf16[1,64,256]{2,1,0:T(8,128)(2,1)S(1)}, u32[]{:S(2)}, u32[]{:S(2)}) collective-permute-start(bf16[1,64,256]{2,1,0:T(8,128)(2,1)S(1)} %bitcast.400), channel_id=1, source_target_pairs={{2,0},{4,2},{6,4},{8,6},{10,8},{12,10},{14,12},{16,14},{18,16},{20... | collective-permute-start | bytes 98312 | tf_op jit(solution)/shard_map/ppermute | solution.py:39
  14.3 111.6 %collective-permute-start.5 = (bf16[1,64,256]{2,1,0:T(8,128)(2,1)S(1)}, bf16[1,64,256]{2,1,0:T(8,128)(2,1)S(1)}, u32[]{:S(2)}, u32[]{:S(2)}) collective-permute-start(bf16[1,64,256]{2,1,0:T(8,128)(2,1)S(1)} %bitcast.401), channel_id=1, source_target_pairs={{8,0},{10,2},{12,4},{14,6},{16,8},{18,10},{20,12},{22,14},{24,16},... | collective-permute-start | bytes 98312 | tf_op jit(solution)/shard_map/ppermute | solution.py:39
  17.6 96.2 %collective-permute-start.1 = (bf16[1,64,256]{2,1,0:T(8,128)(2,1)S(1)}, bf16[1,64,256]{2,1,0:T(8,128)(2,1)S(1)}, u32[]{:S(2)}, u32[]{:S(2)}) collective-permute-start(bf16[1,64,256]{2,1,0:T(8,128)(2,1)S(1)} %bitcast.402), channel_id=1, source_target_pairs={{0,2},{2,4},{4,6},{6,8},{8,10},{10,12},{12,14},{14,16},{16,18},{18... | collective-permute-start | bytes 98312 | tf_op jit(solution)/shard_map/ppermute | solution.py:39
  21.0 99.0 %collective-permute-start = (bf16[1,64,256]{2,1,0:T(8,128)(2,1)S(1)}, bf16[1,64,256]{2,1,0:T(8,128)(2,1)S(1)}, u32[]{:S(2)}, u32[]{:S(2)}) collective-permute-start(bf16[1,64,256]{2,1,0:T(8,128)(2,1)S(1)} %bitcast.403), channel_id=1, source_target_pairs={{0,8},{2,10},{4,12},{6,14},{8,16},{10,18},{12,20},{14,22},{16,24},... | collective-permute-start | bytes 98312 | tf_op jit(solution)/shard_map/ppermute | solution.py:39
  136.8 25.8 %collective-permute-start.7 = (f32[4,64]{1,0:T(4,128)S(1)}, f32[4,64]{1,0:T(4,128)S(1)}, u32[]{:S(2)}, u32[]{:S(2)}) collective-permute-start(f32[4,64]{1,0:T(4,128)S(1)} %get-tuple-element.95), channel_id=1, source_target_pairs={{8,0},{10,2},{12,4},{14,6},{16,8},{18,10},{20,12},{22,14},{24,16},... | collective-permute-start | bytes 3080 | tf_op jit(solution)/shard_map/ppermute | solution.py:39
  138.7 83.4 %collective-permute-start.28 = (f32[4,64]{1,0:T(4,128)S(1)}, f32[4,64]{1,0:T(4,128)S(1)}, u32[]{:S(2)}, u32[]{:S(2)}) collective-permute-start(f32[4,64]{1,0:T(4,128)S(1)} %get-tuple-element.96), channel_id=1, source_target_pairs={{0,8},{2,10},{4,12},{6,14},{8,16},{10,18},{12,20},{14,22},{16,24},... | collective-permute-start | bytes 3080 | tf_op jit(solution)/shard_map/ppermute | solution.py:39
  146.0 21.6 %collective-permute-start.10 = (f32[4,64]{1,0:T(4,128)S(1)}, f32[4,64]{1,0:T(4,128)S(1)}, u32[]{:S(2)}, u32[]{:S(2)}) collective-permute-start(f32[4,64]{1,0:T(4,128)S(1)} %get-tuple-element.102), channel_id=1, source_target_pairs={{6,0},{8,2},{10,4},{12,6},{14,8},{16,10},{18,12},{20,14},{22,16},{... | collective-permute-start | bytes 3080 | tf_op jit(solution)/shard_map/ppermute | solution.py:39
  154.5 23.6 %collective-permute-start.9 = (f32[4,64]{1,0:T(4,128)S(1)}, f32[4,64]{1,0:T(4,128)S(1)}, u32[]{:S(2)}, u32[]{:S(2)}) collective-permute-start(f32[4,64]{1,0:T(4,128)S(1)} %get-tuple-element.110), channel_id=1, source_target_pairs={{6,0},{8,2},{10,4},{12,6},{14,8},{16,10},{18,12},{20,14},{22,16},{... | collective-permute-start | bytes 3080 | tf_op jit(solution)/shard_map/ppermute | solution.py:39
  162.5 54.4 %collective-permute-start.25 = (f32[4,64]{1,0:T(4,128)S(1)}, f32[4,64]{1,0:T(4,128)S(1)}, u32[]{:S(2)}, u32[]{:S(2)}) collective-permute-start(f32[4,64]{1,0:T(4,128)S(1)} %get-tuple-element.97), channel_id=1, source_target_pairs={{0,6},{2,8},{4,10},{6,12},{8,14},{10,16},{12,18},{14,20},{16,22},{... | collective-permute-start | bytes 3080 | tf_op jit(solution)/shard_map/ppermute | solution.py:39
  167.6 35.7 %collective-permute-start.22 = (f32[4,64]{1,0:T(4,128)S(1)}, f32[4,64]{1,0:T(4,128)S(1)}, u32[]{:S(2)}, u32[]{:S(2)}) collective-permute-start(f32[4,64]{1,0:T(4,128)S(1)} %get-tuple-element.98), channel_id=1, source_target_pairs={{0,4},{2,6},{4,8},{6,10},{8,12},{10,14},{12,16},{14,18},{16,20},{1... | collective-permute-start | bytes 3080 | tf_op jit(solution)/shard_map/ppermute | solution.py:39
  198.3 25.7 %collective-permute-start.27 = (f32[4,64]{1,0:T(4,128)}, f32[4,64]{1,0:T(4,128)S(1)}, u32[]{:S(2)}, u32[]{:S(2)}) collective-permute-start(f32[4,64]{1,0:T(4,128)} %get-tuple-element.104), channel_id=1, source_target_pairs={{0,8},{2,10},{4,12},{6,14},{8,16},{10,18},{12,20},{14,22},{16,24},... | collective-permute-start | bytes 3080 | tf_op jit(solution)/shard_map/ppermute | solution.py:39
  222.0 29.5 %collective-permute-start.23 = (f32[64,256]{1,0:T(8,128)}, f32[64,256]{1,0:T(8,128)}, u32[]{:S(2)}, u32[]{:S(2)}) collective-permute-start(f32[64,256]{1,0:T(8,128)} %get-tuple-element.66), channel_id=1, source_target_pairs={{0,4},{2,6},{4,8},{6,10},{8,12},{10,14},{12,16},{14,18},{16,20},{1... | collective-permute-start | bytes 196616 | tf_op jit(solution)/shard_map/ppermute | solution.py:39
  224.0 27.6 %collective-permute-start.20 = (f32[64,256]{1,0:T(8,128)}, f32[64,256]{1,0:T(8,128)}, u32[]{:S(2)}, u32[]{:S(2)}) collective-permute-start(f32[64,256]{1,0:T(8,128)} %get-tuple-element.67), channel_id=1, source_target_pairs={{0,2},{2,4},{4,6},{6,8},{8,10},{10,12},{12,14},{14,16},{16,18},{18... | collective-permute-start | bytes 196616 | tf_op jit(solution)/shard_map/ppermute | solution.py:39
  226.2 25.4 %collective-permute-start.17 = (f32[64,256]{1,0:T(8,128)}, f32[64,256]{1,0:T(8,128)}, u32[]{:S(2)}, u32[]{:S(2)}) collective-permute-start(f32[64,256]{1,0:T(8,128)} %get-tuple-element.68), channel_id=1, source_target_pairs={{2,0},{4,2},{6,4},{8,6},{10,8},{12,10},{14,12},{16,14},{18,16},{20... | collective-permute-start | bytes 196616 | tf_op jit(solution)/shard_map/ppermute | solution.py:39
  278.8 31.3 %collective-permute-start.35 = (bf16[1,64,256]{2,1,0:T(8,128)(2,1)S(1)}, bf16[1,64,256]{2,1,0:T(8,128)(2,1)S(1)}, u32[]{:S(2)}, u32[]{:S(2)}) collective-permute-start(bf16[1,64,256]{2,1,0:T(8,128)(2,1)S(1)} %bitcast.406), channel_id=1, source_target_pairs={{8,0},{10,2},{12,4},{14,6},{16,8},{18,10},{20,12},{22,14},{24,16},... | collective-permute-start | bytes 98312 | tf_op jit(solution)/shard_map/ppermute | solution.py:39
  321.1 25.2 %collective-permute-start.37 = (f32[4,64]{1,0:T(4,128)S(1)}, f32[4,64]{1,0:T(4,128)S(1)}, u32[]{:S(2)}, u32[]{:S(2)}) collective-permute-start(f32[4,64]{1,0:T(4,128)S(1)} %get-tuple-element.79), channel_id=1, source_target_pairs={{8,0},{10,2},{12,4},{14,6},{16,8},{18,10},{20,12},{22,14},{24,16},... | collective-permute-start | bytes 3080 | tf_op jit(solution)/shard_map/ppermute | solution.py:39
  323.1 84.1 %collective-permute-start.58 = (f32[4,64]{1,0:T(4,128)S(1)}, f32[4,64]{1,0:T(4,128)S(1)}, u32[]{:S(2)}, u32[]{:S(2)}) collective-permute-start(f32[4,64]{1,0:T(4,128)S(1)} %get-tuple-element.80), channel_id=1, source_target_pairs={{0,8},{2,10},{4,12},{6,14},{8,16},{10,18},{12,20},{14,22},{16,24},... | collective-permute-start | bytes 3080 | tf_op jit(solution)/shard_map/ppermute | solution.py:39
  338.3 23.6 %collective-permute-start.39 = (f32[4,64]{1,0:T(4,128)S(1)}, f32[4,64]{1,0:T(4,128)S(1)}, u32[]{:S(2)}, u32[]{:S(2)}) collective-permute-start(f32[4,64]{1,0:T(4,128)S(1)} %get-tuple-element.94), channel_id=1, source_target_pairs={{6,0},{8,2},{10,4},{12,6},{14,8},{16,10},{18,12},{20,14},{22,16},{... | collective-permute-start | bytes 3080 | tf_op jit(solution)/shard_map/ppermute | solution.py:39
  346.3 55.4 %collective-permute-start.55 = (f32[4,64]{1,0:T(4,128)S(1)}, f32[4,64]{1,0:T(4,128)S(1)}, u32[]{:S(2)}, u32[]{:S(2)}) collective-permute-start(f32[4,64]{1,0:T(4,128)S(1)} %get-tuple-element.81), channel_id=1, source_target_pairs={{0,6},{2,8},{4,10},{6,12},{8,14},{10,16},{12,18},{14,20},{16,22},{... | collective-permute-start | bytes 3080 | tf_op jit(solution)/shard_map/ppermute | solution.py:39
  351.5 36.9 %collective-permute-start.52 = (f32[4,64]{1,0:T(4,128)S(1)}, f32[4,64]{1,0:T(4,128)S(1)}, u32[]{:S(2)}, u32[]{:S(2)}) collective-permute-start(f32[4,64]{1,0:T(4,128)S(1)} %get-tuple-element.82), channel_id=1, source_target_pairs={{0,4},{2,6},{4,8},{6,10},{8,12},{10,14},{12,16},{14,18},{16,20},{1... | collective-permute-start | bytes 3080 | tf_op jit(solution)/shard_map/ppermute | solution.py:39
  383.1 26.0 %collective-permute-start.57 = (f32[4,64]{1,0:T(4,128)S(1)}, f32[4,64]{1,0:T(4,128)S(1)}, u32[]{:S(2)}, u32[]{:S(2)}) collective-permute-start(f32[4,64]{1,0:T(4,128)S(1)} %get-tuple-element.88), channel_id=1, source_target_pairs={{0,8},{2,10},{4,12},{6,14},{8,16},{10,18},{12,20},{14,22},{16,24},... | collective-permute-start | bytes 3080 | tf_op jit(solution)/shard_map/ppermute | solution.py:39
  407.1 32.1 %collective-permute-start.53 = (f32[64,256]{1,0:T(8,128)}, f32[64,256]{1,0:T(8,128)}, u32[]{:S(2)}, u32[]{:S(2)}) collective-permute-start(f32[64,256]{1,0:T(8,128)} %get-tuple-element.58), channel_id=1, source_target_pairs={{0,4},{2,6},{4,8},{6,10},{8,12},{10,14},{12,16},{14,18},{16,20},{1... | collective-permute-start | bytes 196616 | tf_op jit(solution)/shard_map/ppermute | solution.py:39
  409.1 30.2 %collective-permute-start.50 = (f32[64,256]{1,0:T(8,128)}, f32[64,256]{1,0:T(8,128)}, u32[]{:S(2)}, u32[]{:S(2)}) collective-permute-start(f32[64,256]{1,0:T(8,128)} %get-tuple-element.59), channel_id=1, source_target_pairs={{0,2},{2,4},{4,6},{6,8},{8,10},{10,12},{12,14},{14,16},{16,18},{18... | collective-permute-start | bytes 196616 | tf_op jit(solution)/shard_map/ppermute | solution.py:39
  411.3 28.0 %collective-permute-start.47 = (f32[64,256]{1,0:T(8,128)}, f32[64,256]{1,0:T(8,128)}, u32[]{:S(2)}, u32[]{:S(2)}) collective-permute-start(f32[64,256]{1,0:T(8,128)} %get-tuple-element.60), channel_id=1, source_target_pairs={{2,0},{4,2},{6,4},{8,6},{10,8},{12,10},{14,12},{16,14},{18,16},{20... | collective-permute-start | bytes 196616 | tf_op jit(solution)/shard_map/ppermute | solution.py:39
  (59 other events, 1028.6 us)
where the time goes:
time: 466 us; the launch traced here: 457 us
  starting transfers between devices  230 us (49%)
  blocking collectives  61.9 us (13%)
  local copies, waits for them, and re-layouts  46.9 us (10%)
  matrix products  41.9 us (9%)
  waiting for transfers between devices  37.3 us (8%)
  other arithmetic  36.1 us (8%)
    ppermute x60, starting transfers between devices, passed_along(): lax.ppermute(value, axis, [(source, source + steps) for source in range(i...  230 us
    ppermute x60, waiting for transfers between devices, passed_along(): lax.ppermute(value, axis, [(source, source + steps) for source in range(i...  37.3 us
    all_to_all x2, blocking collectives, copy_for_each(): return lax.all_to_all(copies, axis, split_axis=0, concat_axis=0, tiled=True)  36.6 us
    all_gather x3, blocking collectives, entering(): pieces = lax.all_gather(running, axis)  25.3 us
    reshape x2, local copies, waits for them, and re-layouts, local(): keys.reshape(frames, patches, heads, HEAD_DIM)  14.5 us
    dot_general x4, matrix products, block_stats(): jnp.einsum('bqhd,bkhd->bhqk', queries, keys, preferred_element_type=jnp.f...  11.9 us
    mul x72, local copies, waits for them, and re-layouts, weigh_acc(): scaled = shaped * jnp.swapaxes(weight, -1, -2)[..., None]  11.5 us
    convert_element_type x1, other arithmetic, local(): (unit * media_gain[layer]).astype(jnp.bfloat16)  10.6 us
  transfers between devices with their start and end apart: 60, of which 9 were waited for; matrix products, arithmetic and copies ran while one was open for 20% of the time, Pallas kernels for 0%

commit v1 on v0

v1 whole, which is shorter than its diff:
```python
import functools

import jax
import jax.numpy as jnp
from jax import lax
from jax.experimental import pallas as pl
from jax.experimental.pallas import tpu as pltpu
from jax.sharding import PartitionSpec as P

MESH = pl.DeviceIdType.MESH
HEAD_DIM = 64
LAYERS = 2
REACH = 4
SPAN = 2 * REACH + 1
BACK = 2 * REACH
EPS = 1e-05
FLOOR = -1e30
EARLY = 10
ORDER = (0, 8, 1, 7, 2, 6, 3, 5)

f32 = jnp.float32
bf16 = jnp.bfloat16


def normalize(values):
    mean = jnp.mean(values, axis=-1, keepdims=True)
    center = values - mean
    spread = jnp.mean(center * center, axis=-1, keepdims=True)
    return center * lax.rsqrt(spread + EPS)


def dot(a, b):
    return jnp.dot(a, b, preferred_element_type=f32)


def rows_to_lanes(tall, heads):
    rows = tall.shape[0] // heads
    return jnp.concatenate([tall[h * rows : (h + 1) * rows] for h in range(heads)], axis=1)


def kernel(
    n_dp,
    clip_s,
    clip_h,
    media_h,
    table_h,
    latents_h,
    mgain_h,
    lgain_h,
    fgain_h,
    wq_h,
    wk_h,
    wv_h,
    wo_h,
    out_ref,
    clip_v,
    near_clips,
    media,
    table,
    latents,
    mgain,
    lgain,
    fgain,
    wq,
    wkv,
    wo,
    stamps,
    norm_a,
    norm_b,
    norm1,
    k_a,
    k_b,
    v_a,
    v_b,
    k1,
    v1,
    accs,
    tops,
    totals,
    q_near,
    q_wide,
    part_acc,
    part_st,
    got_acc,
    got_st,
    attn_all,
    self_acc,
    self_st,
    state,
    local_sem,
    media_sem,
    clip_send,
    clip_recv,
    wo_send,
    wo_recv,
    acc_send,
    acc_recv,
    st_send,
    st_recv,
    q_send,
    q_recv,
    at_send,
    at_recv,
):
    frames, patches, width = media.shape
    inner = wq.shape[2]
    heads = inner // HEAD_DIM
    lat = latents.shape[0]
    hq = heads * lat
    me = lax.axis_index("dp")
    core = lax.axis_index("mp")

    def at(step):
        return (lax.rem(me + step + n_dp, n_dp), core)

    partner = (me, 1 - core)

    barrier = pltpu.get_barrier_semaphore()
    for step in range(1, BACK + 1):
        pl.semaphore_signal(barrier, inc=1, device_id=at(step), device_id_type=MESH)
        pl.semaphore_signal(barrier, inc=1, device_id=at(-step), device_id_type=MESH)
    pl.semaphore_signal(barrier, inc=1, device_id=partner, device_id_type=MESH)

    mine = pl.ds(pl.multiple_of(core * inner, inner), inner)
    loads = [
        (clip_h, clip_v),
        (latents_h, latents),
        (lgain_h, lgain),
        (mgain_h, mgain),
        (fgain_h, fgain),
        (wq_h, wq),
        (wk_h, wkv.at[:, :, pl.ds(0, inner)]),
        (wv_h, wkv.at[:, :, pl.ds(inner, inner)]),
        (table_h, table),
        (wo_h, wo.at[:, mine, :]),
    ]
    loads = [pltpu.make_async_copy(a, b, local_sem.at[i]) for i, (a, b) in enumerate(loads)]
    for copy in loads:
        copy.start()
    media_in = [pltpu.make_async_copy(media_h.at[f], media.at[f], media_sem.at[f]) for f in range(frames)]
    for copy in media_in:
        copy.start()

    loads[0].wait()
    pl.semaphore_wait(barrier, 2 * BACK + 1)
    clip_copies = [
        pltpu.make_async_remote_copy(
            src_ref=clip_v,
            dst_ref=near_clips.at[step - 1],
            send_sem=clip_send.at[step - 1],
            recv_sem=clip_recv.at[step - 1],
            device_id=at(step),
            device_id_type=MESH,
        )
        for step in range(1, BACK + 1)
    ]
    for copy in clip_copies[::-1]:
        copy.start()
    wo_copy = pltpu.make_async_remote_copy(
        src_ref=wo_h,
        dst_ref=wo.at[:, mine, :],
        send_sem=wo_send,
        recv_sem=wo_recv,
        device_id=partner,
        device_id_type=MESH,
    )
    wo_copy.start()

    row_head = lax.broadcasted_iota(jnp.int32, (inner, hq), 0) // HEAD_DIM
    lane_head = lax.broadcasted_iota(jnp.int32, (inner, hq), 1) // lat
    same_head = row_head == lane_head
    piece_head = lax.broadcasted_iota(jnp.int32, (HEAD_DIM, hq), 1) // lat

    def widen(compact):
        tiled = jnp.concatenate([compact] * heads, axis=0)
        return jnp.where(same_head, tiled, jnp.zeros_like(tiled))

    def block(keys, values, wide):
        scores = dot(keys, wide)
        top = jnp.max(scores, axis=0, keepdims=True)
        expo = jnp.exp(scores - top)
        total = jnp.sum(expo, axis=0, keepdims=True)
        full = lax.dot_general(
            values, expo.astype(bf16), (((0,), (0,)), ((), ())), preferred_element_type=f32
        )
        acc = full[0:HEAD_DIM]
        for h in range(1, heads):
            acc = jnp.where(piece_head == h, full[h * HEAD_DIM : (h + 1) * HEAD_DIM], acc)
        return top, total, acc

    def latent_side(layer):
        lat_norm = (normalize(state[...]) * lgain[layer : layer + 1, :]).astype(bf16)
        query = dot(lat_norm, wq[layer]) * (HEAD_DIM ** (-0.5))
        compact = rows_to_lanes(query.T, heads).astype(bf16)
        q_near[layer, REACH] = compact
        return lat_norm, compact

    def self_block(layer, lat_norm, compact):
        kv = dot(lat_norm, wkv[layer]).astype(bf16)
        top, total, acc = block(kv[:, :inner], kv[:, inner:], widen(compact))
        self_st[0:1, :] = top
        self_st[1:2, :] = total
        self_acc[...] = acc

    for copy in loads[1:9]:
        copy.wait()
    state[...] = latents[...]
    lat_norm, compact = latent_side(0)
    self_block(0, lat_norm, compact)
    q_wide[REACH] = widen(compact)

    row = lax.broadcasted_iota(jnp.int32, (frames, frames), 0)
    lane = lax.broadcasted_iota(jnp.int32, (frames, frames), 1)
    clip_col = jnp.zeros((frames, 1), jnp.int32)
    frame_row = lax.broadcasted_iota(jnp.int32, (frames, 1), 0)
    for f in range(frames):
        clip_col = jnp.where(frame_row == f, clip_s[f], clip_col)
    slot_col = clip_col - me + REACH
    own_row = clip_v[...]
    seen = jnp.where((clip_col == own_row) & (lane < row), 1.0, 0.0)
    for step in range(1, BACK + 1):
        clip_copies[step - 1].wait_recv()
        seen += jnp.where(clip_col == near_clips[step - 1], 1.0, 0.0)
    index = jnp.sum(seen, axis=1, keepdims=True).astype(jnp.int32)
    times = table.shape[0]
    picker = (lax.broadcasted_iota(jnp.int32, (frames, times), 1) == index).astype(f32).astype(bf16)
    stamps[...] = dot(picker, table[...])

    chunk = 16

    def norm_frame(f, dst):
        stamp = stamps[pl.ds(f, 1), :]
        for r in range(patches // chunk):
            rows = slice(r * chunk, (r + 1) * chunk)
            unit = normalize(media[f, rows, :].astype(f32) + stamp)
            dst[rows, :] = (unit * mgain[0:1, :]).astype(bf16)
            norm1[f, rows, :] = (unit * mgain[1:2, :]).astype(bf16)

    def project(src, k_dst, v_dst):
        kv = dot(src[...], wkv[0]).astype(bf16)
        k_dst[...] = kv[:, :inner]
        v_dst[...] = kv[:, inner:]

    def project1(f):
        kv = dot(norm1[f], wkv[1]).astype(bf16)
        k1[f] = kv[:, :inner]
        v1[f] = kv[:, inner:]

    def attend(f, keys, values, wide):
        top, total, acc = block(keys, values, wide)
        tops[pl.ds(f, 1), :] = top
        totals[pl.ds(f, 1), :] = total
        accs[f] = acc

    def media_wait(f):
        pltpu.make_async_copy(media_h.at[f], media.at[f], media_sem.at[f]).wait()

    wide0 = q_wide.at[REACH]
    media_wait(0)
    norm_frame(0, norm_a)
    media_wait(1)
    norm_frame(1, norm_b)
    project(norm_a, k_a, v_a)

    def pair(i, carry):
        f = 2 * i
        media_wait(f)
        media_wait(f + 1)
        norm_frame(f, norm_a)
        project(norm_b, k_b, v_b)
        attend(f - 2, k_a[...], v_a[...], wide0[...])
        norm_frame(f + 1, norm_b)
        project(norm_a, k_a, v_a)
        attend(f - 1, k_b[...], v_b[...], wide0[...])
        return carry

    lax.fori_loop(1, frames // 2, pair, 0)
    project(norm_b, k_b, v_b)
    attend(frames - 2, k_a[...], v_a[...], wide0[...])
    attend(frames - 1, k_b[...], v_b[...], wide0[...])

    def gather_part(layer, slot):
        chosen = slot_col == slot
        top = jnp.max(jnp.where(chosen, tops[...], FLOOR), axis=0, keepdims=True)
        weight = jnp.where(chosen, jnp.exp(jnp.where(chosen, tops[...] - top, 0.0)), 0.0)
        total = jnp.sum(weight * totals[...], axis=0, keepdims=True)
        acc = jnp.zeros((HEAD_DIM, hq), f32)
        for f in range(frames):
            acc += weight[f : f + 1, :] * accs[f]
        part_acc[layer, slot] = acc.astype(bf16)
        part_st[layer, slot, 0:1, :] = top
        part_st[layer, slot, 1:2, :] = total

    def part_copies(layer, slot):
        to = at(slot - REACH)
        return (
            pltpu.make_async_remote_copy(
                src_ref=part_st.at[layer, slot],
                dst_ref=got_st.at[layer, slot],
                send_sem=st_send.at[layer, slot],
                recv_sem=st_recv.at[layer, slot],
                device_id=to,
                device_id_type=MESH,
            ),
            pltpu.make_async_remote_copy(
                src_ref=part_acc.at[layer, slot],
                dst_ref=got_acc.at[layer, slot],
                send_sem=acc_send.at[layer, slot],
                recv_sem=acc_recv.at[layer, slot],
                device_id=to,
                device_id_type=MESH,
            ),
        )

    def send_parts(layer):
        for slot in ORDER:
            gather_part(layer, slot)
            for copy in part_copies(layer, slot):
                copy.start()
        gather_part(layer, REACH)

    def merge_parts(layer):
        for slot in ORDER:
            for copy in part_copies(layer, slot):
                copy.wait_recv()
        sources = [(self_st[0:1, :], self_st[1:2, :], self_acc)]
        sources.append((part_st[layer, REACH, 0:1, :], part_st[layer, REACH, 1:2, :], part_acc.at[layer, REACH]))
        for slot in ORDER:
            sources.append((got_st[layer, slot, 0:1, :], got_st[layer, slot, 1:2, :], got_acc.at[layer, slot]))
        best = functools.reduce(jnp.maximum, [top for top, _, _ in sources])
        whole = jnp.zeros_like(best)
        combined = jnp.zeros((HEAD_DIM, hq), f32)
        for top, total, acc in sources:
            weight = jnp.exp(top - best)
            whole += weight * total
            combined += weight * acc[...].astype(f32)
        return rows_to_lanes((combined / whole).T, heads).astype(bf16)

    def update_state(layer):
        attn_all[layer, :, mine] = merge_parts(layer)
        copy = pltpu.make_async_remote_copy(
            src_ref=attn_all.at[layer, :, mine],
            dst_ref=attn_all.at[layer, :, mine],
            send_sem=at_send.at[layer],
            recv_sem=at_recv.at[layer],
            device_id=partner,
            device_id_type=MESH,
        )
        copy.start()
        copy.wait_recv()
        state[...] += dot(attn_all[layer], wo[layer])
        return copy

    def loop1(start, stop):
        def step(f, carry):
            project1(f)
            return carry

        lax.fori_loop(start, stop, step, 0)

    send_parts(0)
    loop1(0, EARLY)
    loads[9].wait()
    wo_copy.wait()
    at0 = update_state(0)

    lat_norm, compact = latent_side(1)
    q_copies = [
        pltpu.make_async_remote_copy(
            src_ref=q_near.at[1, REACH],
            dst_ref=q_near.at[1, REACH - (slot - REACH)],
            send_sem=q_send.at[slot],
            recv_sem=q_recv.at[REACH - (slot - REACH)],
            device_id=at(slot - REACH),
            device_id_type=MESH,
        )
        for slot in ORDER
    ]
    for copy in q_copies:
        copy.start()
    self_block(1, lat_norm, compact)
    loop1(EARLY, frames)
    q_wide[REACH] = widen(compact)
    for slot, copy in zip(ORDER, q_copies):
        copy.wait_recv()
        q_wide[SPAN - 1 - slot] = widen(q_near[1, SPAN - 1 - slot])

    def attend1(i, carry):
        for f in (2 * i, 2 * i + 1):
            attend(f, k1[f], v1[f], q_wide[jnp.clip(clip_s[f] - me + REACH, 0, SPAN - 1)])
        return carry

    lax.fori_loop(0, frames // 2, attend1, 0)
    send_parts(1)
    at1 = update_state(1)
    out_ref[...] = normalize(state[...]) * fgain[...]

    for copy in clip_copies:
        copy.wait_send()
    for layer in range(LAYERS):
        for slot in ORDER:
            for copy in part_copies(layer, slot):
                copy.wait_send()
    for copy in q_copies:
        copy.wait_send()
    at0.wait_send()
    at1.wait_send()


def local(n_dp, media, slot_clip, table, latents, mgain, lgain, fgain, wq, wk, wv, wo):
    frames, patches, width = media.shape
    layers, _, inner = wq.shape
    heads = inner // HEAD_DIM
    lat = latents.shape[0]
    hq = heads * lat
    vmem, dma = pltpu.VMEM, pltpu.SemaphoreType.DMA
    scratch = [
        vmem((1, frames), jnp.int32),
        vmem((BACK, 1, frames), jnp.int32),
        vmem((frames, patches, width), bf16),
        vmem(table.shape, bf16),
        vmem(latents.shape, f32),
        vmem(mgain.shape, f32),
        vmem(lgain.shape, f32),
        vmem((1, width), f32),
        vmem(wq.shape, bf16),
        vmem((layers, width, 2 * inner), bf16),
        vmem((layers, 2 * inner, width), bf16),
        vmem((frames, width), f32),
        vmem((patches, width), bf16),
        vmem((patches, width), bf16),
        vmem((frames, patches, width), bf16),
        vmem((patches, inner), bf16),
        vmem((patches, inner), bf16),
        vmem((patches, inner), bf16),
        vmem((patches, inner), bf16),
        vmem((frames, patches, inner), bf16),
        vmem((frames, patches, inner), bf16),
        vmem((frames, HEAD_DIM, hq), f32),
        vmem((frames, hq), f32),
        vmem((frames, hq), f32),
        vmem((layers, SPAN, HEAD_DIM, hq), bf16),
        vmem((SPAN, inner, hq), bf16),
        vmem((layers, SPAN, HEAD_DIM, hq), bf16),
        vmem((layers, SPAN, 2, hq), f32),
        vmem((layers, SPAN, HEAD_DIM, hq), bf16),
        vmem((layers, SPAN, 2, hq), f32),
        vmem((layers, lat, 2 * inner), bf16),
        vmem((HEAD_DIM, hq), f32),
        vmem((2, hq), f32),
        vmem(latents.shape, f32),
        dma((10,)),
        dma((frames,)),
        dma((BACK,)),
        dma((BACK,)),
        dma(()),
        dma(()),
        dma((layers, SPAN)),
        dma((layers, SPAN)),
        dma((layers, SPAN)),
        dma((layers, SPAN)),
        dma((SPAN,)),
        dma((SPAN,)),
        dma((layers,)),
        dma((layers,)),
    ]
    result = pl.pallas_call(
        functools.partial(kernel, n_dp),
        out_shape=jax.ShapeDtypeStruct(latents.shape, f32),
        in_specs=[pl.BlockSpec(memory_space=pltpu.SMEM)] + [pl.BlockSpec(memory_space=pl.ANY)] * 11,
        out_specs=pl.BlockSpec(memory_space=pltpu.VMEM),
        scratch_shapes=scratch,
        compiler_params=pltpu.CompilerParams(
            collective_id=0, has_side_effects=True, vmem_limit_bytes=60 * 1024 * 1024
        ),
        name="resample",
    )(slot_clip, slot_clip[None, :], media, table, latents, mgain, lgain, fgain[None, :], wq, wk, wv, wo)
    return result[None]


def solution(mesh):
    return jax.shard_map(
        functools.partial(local, mesh.shape["dp"]),
        mesh=mesh,
        in_specs=(
            P("dp", None, None),
            P("dp"),
            P(),
            P(),
            P(),
            P(),
            P(),
            P(None, None, "mp"),
            P(None, None, "mp"),
            P(None, None, "mp"),
            P(None, "mp", None),
        ),
        out_specs=P("dp", None, None),
        check_vma=False,
    )
```

time: 466 us -> 73.9 us (0.16)
  the two profiles are of different devices: /device:TPU:25 before, /device:TPU:1 now
where the time goes in v1:
time: 73.9 us; the launch traced here: 73.7 us
  Pallas kernels  72.1 us (98%)
  local copies, waits for them, and re-layouts  1.67 us (2%)
    pallas_call x1, Pallas kernels, local(): pl.pallas_call(functools.partial(kernel, n_dp), out_shape=jax.ShapeDtypeS...  72.1 us
    unnamed x1, local copies, waits for them, and re-layouts  1.67 us

profile of v1, /device:TPU:1, one launch (start us, length us, event | category | flops | bytes accessed | tf_op | source)
XLA Modules:
  0.0 73.7 jit_solution(17210256774812310607)
XLA Ops:
  0.0 72.1 %resample.1 = f32[64,1024]{1,0:T(8,128)} custom-call(s32[16]{0:T(128)} %clip_s.1, s32[1,16]{1,0:T(1,128)} %bitcast.5, bf16[16,256,1024]{2,1,0:T(8,128)(2,1)} %media_h.1, bf16[144,1024]{1,0:T(8,128)(2,1)} %table_h.1, f32[64,1024]{1,0:T(8,128)} %latents_h.1, f32[2,1024]{1,0:T(2,128)} %mgain_h.1, f32[2,1024]{1,0:T(2,128)} %lgain_h.1, f32[1,1024]{1,0:T(1,128)} %bitcast.4, ...), custom_call_target="tpu_custom_call" | custom-call | tf_op jit(solution)/shard_map/resample/pallas_call | solution.py:467
  72.1 1.7 %copy.13 = f32[1,64,1024]{2,1,0:T(8,128)} copy(f32[1,64,1024]{2,1,0:T(8,128)} %bitcast.3) | data formatting | bytes 524288

commit v2 on v1

--- a/solution.py
+++ b/solution.py
@@ -67,7 +67,8 @@
     stamps,
     norm_a,
     norm_b,
-    norm1,
+    scales,
+    centered,
     k_a,
     k_b,
     v_a,
@@ -78,7 +79,8 @@
     tops,
     totals,
     q_near,
-    q_wide,
+    wide0,
+    diagonal,
     part_acc,
     part_st,
     got_acc,
@@ -111,14 +113,23 @@
     core = lax.axis_index("mp")
 
     def at(step):
-        return (lax.rem(me + step + n_dp, n_dp), core)
+        return (me + step, core)
+
+    def near(step):
+        return pl.when(me + step < n_dp if step > 0 else me + step >= 0)
+
+    def beyond(step):
+        return pl.when(me + step >= n_dp if step > 0 else me + step < 0)
 
     partner = (me, 1 - core)
 
     barrier = pltpu.get_barrier_semaphore()
-    for step in range(1, BACK + 1):
-        pl.semaphore_signal(barrier, inc=1, device_id=at(step), device_id_type=MESH)
-        pl.semaphore_signal(barrier, inc=1, device_id=at(-step), device_id_type=MESH)
+    for step in (*range(-BACK, 0), *range(1, REACH + 1)):
+
+        @near(step)
+        def _():
+            pl.semaphore_signal(barrier, inc=1, device_id=at(step), device_id_type=MESH)
+
     pl.semaphore_signal(barrier, inc=1, device_id=partner, device_id_type=MESH)
 
     mine = pl.ds(pl.multiple_of(core * inner, inner), inner)
@@ -142,7 +153,7 @@
         copy.start()
 
     loads[0].wait()
-    pl.semaphore_wait(barrier, 2 * BACK + 1)
+    pl.semaphore_wait(barrier, jnp.minimum(BACK, n_dp - 1 - me) + jnp.minimum(REACH, me) + 1)
     clip_copies = [
         pltpu.make_async_remote_copy(
             src_ref=clip_v,
@@ -154,8 +165,8 @@
         )
         for step in range(1, BACK + 1)
     ]
-    for copy in clip_copies[::-1]:
-        copy.start()
+    for step in range(BACK, 0, -1):
+        near(step)(clip_copies[step - 1].start)
     wo_copy = pltpu.make_async_remote_copy(
         src_ref=wo_h,
         dst_ref=wo.at[:, mine, :],
@@ -168,12 +179,11 @@
 
     row_head = lax.broadcasted_iota(jnp.int32, (inner, hq), 0) // HEAD_DIM
     lane_head = lax.broadcasted_iota(jnp.int32, (inner, hq), 1) // lat
-    same_head = row_head == lane_head
+    diagonal[...] = (row_head == lane_head).astype(f32).astype(bf16)
     piece_head = lax.broadcasted_iota(jnp.int32, (HEAD_DIM, hq), 1) // lat
 
     def widen(compact):
-        tiled = jnp.concatenate([compact] * heads, axis=0)
-        return jnp.where(same_head, tiled, jnp.zeros_like(tiled))
+        return jnp.concatenate([compact] * heads, axis=0) * diagonal[...]
 
     def block(keys, values, wide):
         scores = dot(keys, wide)
@@ -202,12 +212,42 @@
         self_st[1:2, :] = total
         self_acc[...] = acc
 
+    for step in range(1, BACK + 1):
+
+        @beyond(-step)
+        def _():
+            near_clips[step - 1] = jnp.full(near_clips.shape[1:], -1, jnp.int32)
+
+    for slot in ORDER:
+
+        @beyond(REACH - slot)
+        def _():
+            for layer in range(LAYERS):
+                got_st[layer, slot, 0:1, :] = jnp.full((1, hq), FLOOR, f32)
+                got_st[layer, slot, 1:2, :] = jnp.zeros((1, hq), f32)
+                got_acc[layer, slot] = jnp.zeros((HEAD_DIM, hq), bf16)
+
     for copy in loads[1:9]:
         copy.wait()
     state[...] = latents[...]
     lat_norm, compact = latent_side(0)
     self_block(0, lat_norm, compact)
-    q_wide[REACH] = widen(compact)
+    wide0[...] = widen(compact)
+
+    chunk = 16
+
+    def media_wait(f):
+        pltpu.make_async_copy(media_h.at[f], media.at[f], media_sem.at[f]).wait()
+
+    def center(f, carry):
+        media_wait(f)
+        for r in range(patches // chunk):
+            rows = slice(r * chunk, (r + 1) * chunk)
+            x = media[f, rows, :].astype(f32)
+            centered[f, rows, :] = x - jnp.mean(x, axis=-1, keepdims=True)
+        return carry
+
+    lax.fori_loop(0, frames, center, 0)
 
     row = lax.broadcasted_iota(jnp.int32, (frames, frames), 0)
     lane = lax.broadcasted_iota(jnp.int32, (frames, frames), 1)
@@ -219,30 +259,39 @@
     own_row = clip_v[...]
     seen = jnp.where((clip_col == own_row) & (lane < row), 1.0, 0.0)
     for step in range(1, BACK + 1):
-        clip_copies[step - 1].wait_recv()
+        near(-step)(clip_copies[step - 1].wait_recv)
+    for step in range(1, BACK + 1):
         seen += jnp.where(clip_col == near_clips[step - 1], 1.0, 0.0)
     index = jnp.sum(seen, axis=1, keepdims=True).astype(jnp.int32)
     times = table.shape[0]
     picker = (lax.broadcasted_iota(jnp.int32, (frames, times), 1) == index).astype(f32).astype(bf16)
-    stamps[...] = dot(picker, table[...])
-
-    chunk = 16
+    stamp = dot(picker, table[...])
+    stamps[...] = stamp - jnp.mean(stamp, axis=-1, keepdims=True)
 
     def norm_frame(f, dst):
         stamp = stamps[pl.ds(f, 1), :]
         for r in range(patches // chunk):
             rows = slice(r * chunk, (r + 1) * chunk)
-            unit = normalize(media[f, rows, :].astype(f32) + stamp)
-            dst[rows, :] = (unit * mgain[0:1, :]).astype(bf16)
-            norm1[f, rows, :] = (unit * mgain[1:2, :]).astype(bf16)
+            value = centered[f, rows, :] + stamp
+            scale = lax.rsqrt(jnp.mean(value * value, axis=-1, keepdims=True) + EPS)
+            scales[f, rows, :] = jnp.broadcast_to(scale, (chunk, 128))
+            dst[rows, :] = (value * scale * mgain[0:1, :]).astype(bf16)
+
+    def norm_frame1(f, dst):
+        stamp = stamps[pl.ds(f, 1), :]
+        for r in range(patches // chunk):
+            rows = slice(r * chunk, (r + 1) * chunk)
+            value = centered[f, rows, :] + stamp
+            scale = jnp.concatenate([scales[f, rows, :]] * (width // 128), axis=1)
+            dst[rows, :] = (value * scale * mgain[1:2, :]).astype(bf16)
 
     def project(src, k_dst, v_dst):
         kv = dot(src[...], wkv[0]).astype(bf16)
         k_dst[...] = kv[:, :inner]
         v_dst[...] = kv[:, inner:]
 
-    def project1(f):
-        kv = dot(norm1[f], wkv[1]).astype(bf16)
+    def project1(src, f):
+        kv = dot(src[...], wkv[1]).astype(bf16)
         k1[f] = kv[:, :inner]
         v1[f] = kv[:, inner:]
 
@@ -252,20 +301,12 @@
         totals[pl.ds(f, 1), :] = total
         accs[f] = acc
 
-    def media_wait(f):
-        pltpu.make_async_copy(media_h.at[f], media.at[f], media_sem.at[f]).wait()
-
-    wide0 = q_wide.at[REACH]
-    media_wait(0)
     norm_frame(0, norm_a)
-    media_wait(1)
     norm_frame(1, norm_b)
     project(norm_a, k_a, v_a)
 
     def pair(i, carry):
         f = 2 * i
-        media_wait(f)
-        media_wait(f + 1)
         norm_frame(f, norm_a)
         project(norm_b, k_b, v_b)
         attend(f - 2, k_a[...], v_a[...], wide0[...])
@@ -316,13 +357,13 @@
         for slot in ORDER:
             gather_part(layer, slot)
             for copy in part_copies(layer, slot):
-                copy.start()
+                near(slot - REACH)(copy.start)
         gather_part(layer, REACH)
 
     def merge_parts(layer):
         for slot in ORDER:
             for copy in part_copies(layer, slot):
-                copy.wait_recv()
+                near(REACH - slot)(copy.wait_recv)
         sources = [(self_st[0:1, :], self_st[1:2, :], self_acc)]
         sources.append((part_st[layer, REACH, 0:1, :], part_st[layer, REACH, 1:2, :], part_acc.at[layer, REACH]))
         for slot in ORDER:
@@ -352,13 +393,18 @@
         return copy
 
     def loop1(start, stop):
-        def step(f, carry):
-            project1(f)
+        def pair1(i, carry):
+            f = 2 * i
+            norm_frame1(f + 1, norm_b)
+            project1(norm_a, f)
+            norm_frame1(jnp.minimum(f + 2, frames - 1), norm_a)
+            project1(norm_b, f + 1)
             return carry
 
-        lax.fori_loop(start, stop, step, 0)
+        lax.fori_loop(start // 2, stop // 2, pair1, 0)
 
     send_parts(0)
+    norm_frame1(0, norm_a)
     loop1(0, EARLY)
     loads[9].wait()
     wo_copy.wait()
@@ -376,33 +422,36 @@
         )
         for slot in ORDER
     ]
-    for copy in q_copies:
-        copy.start()
+    for slot, copy in zip(ORDER, q_copies):
+        near(slot - REACH)(copy.start)
     self_block(1, lat_norm, compact)
     loop1(EARLY, frames)
-    q_wide[REACH] = widen(compact)
     for slot, copy in zip(ORDER, q_copies):
-        copy.wait_recv()
-        q_wide[SPAN - 1 - slot] = widen(q_near[1, SPAN - 1 - slot])
+        near(REACH - slot)(copy.wait_recv)
 
     def attend1(i, carry):
-        for f in (2 * i, 2 * i + 1):
-            attend(f, k1[f], v1[f], q_wide[jnp.clip(clip_s[f] - me + REACH, 0, SPAN - 1)])
+        for j in range(4):
+            f = 4 * i + j
+            slot = jnp.clip(clip_s[f] - me + REACH, 0, SPAN - 1)
+            attend(f, k1[f], v1[f], widen(q_near[1, slot]))
         return carry
 
-    lax.fori_loop(0, frames // 2, attend1, 0)
+    lax.fori_loop(0, frames // 4, attend1, 0)
     send_parts(1)
     at1 = update_state(1)
     out_ref[...] = normalize(state[...]) * fgain[...]
 
-    for copy in clip_copies:
-        copy.wait_send()
-    for layer in range(LAYERS):
-        for slot in ORDER:
-            for copy in part_copies(layer, slot):
-                copy.wait_send()
-    for copy in q_copies:
-        copy.wait_send()
+    for step in range(1, BACK + 1):
+        near(step)(clip_copies[step - 1].wait_send)
+    for slot, q_copy in zip(ORDER, q_copies):
+
+        @near(slot - REACH)
+        def _():
+            q_copy.wait_send()
+            for layer in range(LAYERS):
+                for copy in part_copies(layer, slot):
+                    copy.wait_send()
+
     at0.wait_send()
     at1.wait_send()
 
@@ -429,7 +478,8 @@
         vmem((frames, width), f32),
         vmem((patches, width), bf16),
         vmem((patches, width), bf16),
-        vmem((frames, patches, width), bf16),
+        vmem((frames, patches, 128), f32),
+        vmem((frames, patches, width), f32),
         vmem((patches, inner), bf16),
         vmem((patches, inner), bf16),
         vmem((patches, inner), bf16),
@@ -440,7 +490,8 @@
         vmem((frames, hq), f32),
         vmem((frames, hq), f32),
         vmem((layers, SPAN, HEAD_DIM, hq), bf16),
-        vmem((SPAN, inner, hq), bf16),
+        vmem((inner, hq), bf16),
+        vmem((inner, hq), bf16),
         vmem((layers, SPAN, HEAD_DIM, hq), bf16),
         vmem((layers, SPAN, 2, hq), f32),
         vmem((layers, SPAN, HEAD_DIM, hq), bf16),

time: 73.9 us -> 68.4 us (0.926)
  the two profiles are of different devices: /device:TPU:1 before, /device:TPU:25 now
where the time goes in v2:
time: 68.4 us; the launch traced here: 68.3 us
  Pallas kernels  66.6 us (97%)
  local copies, waits for them, and re-layouts  1.67 us (2%)
    pallas_call x1, Pallas kernels, local(): pl.pallas_call(functools.partial(kernel, n_dp), out_shape=jax.ShapeDtypeS...  66.6 us
    unnamed x1, local copies, waits for them, and re-layouts  1.67 us

profile of v2, /device:TPU:25, one launch (start us, length us, event | category | flops | bytes accessed | tf_op | source)
XLA Modules:
  0.0 68.3 jit_solution(5541819019036433705)
XLA Ops:
  0.0 66.6 %resample.1 = f32[64,1024]{1,0:T(8,128)} custom-call(s32[16]{0:T(128)} %clip_s.1, s32[1,16]{1,0:T(1,128)} %bitcast.5, bf16[16,256,1024]{2,1,0:T(8,128)(2,1)} %media_h.1, bf16[144,1024]{1,0:T(8,128)(2,1)} %table_h.1, f32[64,1024]{1,0:T(8,128)} %latents_h.1, f32[2,1024]{1,0:T(2,128)} %mgain_h.1, f32[2,1024]{1,0:T(2,128)} %lgain_h.1, f32[1,1024]{1,0:T(1,128)} %bitcast.4, ...), custom_call_target="tpu_custom_call" | custom-call | tf_op jit(solution)/shard_map/resample/pallas_call | solution.py:518
  66.6 1.7 %copy.13 = f32[1,64,1024]{2,1,0:T(8,128)} copy(f32[1,64,1024]{2,1,0:T(8,128)} %bitcast.3) | data formatting | bytes 524288

commit v3 on v2

v3 whole, which is shorter than its diff:
```python
import functools

import jax
import jax.numpy as jnp
from jax import lax
from jax.experimental import pallas as pl
from jax.experimental.pallas import tpu as pltpu
from jax.sharding import PartitionSpec as P

MESH = pl.DeviceIdType.MESH
HEAD_DIM = 64
LAYERS = 2
REACH = 4
SPAN = 2 * REACH + 1
BACK = 2 * REACH
EPS = 1e-05
FLOOR = -1e30
GROUPS = 2
EARLY = 12
ORDER = (0, 8, 1, 7, 2, 6, 3, 5)

f32 = jnp.float32
bf16 = jnp.bfloat16


def normalize(values):
    mean = jnp.mean(values, axis=-1, keepdims=True)
    center = values - mean
    spread = jnp.mean(center * center, axis=-1, keepdims=True)
    return center * lax.rsqrt(spread + EPS)


def dot(a, b):
    return jnp.dot(a, b, preferred_element_type=f32)


def rows_to_lanes(tall, heads):
    rows = tall.shape[0] // heads
    return jnp.concatenate([tall[h * rows : (h + 1) * rows] for h in range(heads)], axis=1)


def other(slot):
    return slot - (slot > REACH)


def part(g, width):
    return slice(g * width, (g + 1) * width)


def kernel(
    n_dp,
    clip_s,
    clip_h,
    media_h,
    table_h,
    latents_h,
    mgain_h,
    lgain_h,
    fgain_h,
    wq_h,
    wk_h,
    wv_h,
    wo_h,
    out_ref,
    clip_v,
    near_clips,
    media,
    table,
    latents,
    mgain,
    lgain,
    fgain,
    wq,
    wkv,
    wo,
    stamps,
    norm_a,
    norm_b,
    scales,
    centered,
    kv_a,
    kv_b,
    kv0,
    p_a,
    p_b,
    kv1,
    accs,
    tops,
    totals,
    q_near_a,
    q_near_b,
    wide0,
    diagonal,
    part_acc,
    part_st,
    got_acc,
    got_st,
    attn_all,
    self_acc,
    self_st,
    state,
    local_sem,
    media_sem,
    clip_send,
    clip_recv,
    wo_send,
    wo_recv,
    acc_send,
    acc_recv,
    st_send,
    st_recv,
    q_send,
    q_recv,
    at_send,
    at_recv,
):
    frames, patches, width = media.shape
    inner = wq.shape[2]
    heads = inner // HEAD_DIM // GROUPS
    lat = latents.shape[0]
    hq = heads * lat
    hd = heads * HEAD_DIM
    me = lax.axis_index("dp")
    core = lax.axis_index("mp")

    def at(step):
        return (me + step, core)

    def near(step):
        return pl.when(me + step < n_dp if step > 0 else me + step >= 0)

    def beyond(step):
        return pl.when(me + step >= n_dp if step > 0 else me + step < 0)

    partner = (me, 1 - core)
    q_near = (q_near_a, q_near_b)

    barrier = pltpu.get_barrier_semaphore()
    for step in (*range(-BACK, 0), *range(1, REACH + 1)):

        @near(step)
        def _():
            pl.semaphore_signal(barrier, inc=1, device_id=at(step), device_id_type=MESH)

    pl.semaphore_signal(barrier, inc=1, device_id=partner, device_id_type=MESH)

    mine = pl.ds(pl.multiple_of(core * inner, inner), inner)
    step4 = 4

    def media_copy(i):
        rows = pl.ds(i * step4, step4)
        return pltpu.make_async_copy(media_h.at[rows], media.at[rows], media_sem.at[i])

    media_in = [media_copy(i) for i in range(frames // step4)]
    loads = [
        (clip_h, clip_v),
        (table_h, table),
        (latents_h, latents),
        (lgain_h, lgain),
        (mgain_h, mgain),
        (fgain_h, fgain),
        (wq_h, wq),
    ]
    for g in range(GROUPS):
        columns = pl.ds(g * hd, hd)
        loads.append((wk_h.at[:, :, columns], wkv.at[:, :, pl.ds(2 * g * hd, hd)]))
        loads.append((wv_h.at[:, :, columns], wkv.at[:, :, pl.ds((2 * g + 1) * hd, hd)]))
    loads.append((wo_h, wo.at[:, mine, :]))
    loads = [pltpu.make_async_copy(a, b, local_sem.at[i]) for i, (a, b) in enumerate(loads)]
    for copy in [loads[0]] + media_in + loads[1:]:
        copy.start()

    loads[0].wait()
    pl.semaphore_wait(barrier, jnp.minimum(BACK, n_dp - 1 - me) + jnp.minimum(REACH, me) + 1)
    clip_copies = [
        pltpu.make_async_remote_copy(
            src_ref=clip_v,
            dst_ref=near_clips.at[step - 1],
            send_sem=clip_send.at[step - 1],
            recv_sem=clip_recv.at[step - 1],
            device_id=at(step),
            device_id_type=MESH,
        )
        for step in range(1, BACK + 1)
    ]
    for step in range(BACK, 0, -1):
        near(step)(clip_copies[step - 1].start)
    wo_copy = pltpu.make_async_remote_copy(
        src_ref=wo_h,
        dst_ref=wo.at[:, mine, :],
        send_sem=wo_send,
        recv_sem=wo_recv,
        device_id=partner,
        device_id_type=MESH,
    )
    wo_copy.start()

    for step in range(1, BACK + 1):

        @beyond(-step)
        def _():
            near_clips[step - 1] = jnp.full(near_clips.shape[1:], -1, jnp.int32)

    for slot in ORDER:

        @beyond(REACH - slot)
        def _():
            for layer in range(LAYERS):
                for g in range(GROUPS):
                    got_st[layer, slot, 2 * g : 2 * g + 1, :] = jnp.full((1, hq), FLOOR, f32)
                    got_st[layer, slot, 2 * g + 1 : 2 * g + 2, :] = jnp.zeros((1, hq), f32)
                    got_acc[layer, g, slot] = jnp.zeros((HEAD_DIM, hq), bf16)

    chunk = 16

    def center(f, carry):
        for r in range(patches // chunk):
            x = media[f, part(r, chunk), :].astype(f32)
            centered[f, part(r, chunk), :] = x - jnp.mean(x, axis=-1, keepdims=True)
        return carry

    for i in range(frames // step4):
        media_in[i].wait()
        lax.fori_loop(i * step4, (i + 1) * step4, center, 0)

    row_head = lax.broadcasted_iota(jnp.int32, (hd, hq), 0) // HEAD_DIM
    lane_head = lax.broadcasted_iota(jnp.int32, (hd, hq), 1) // lat
    diagonal[...] = (row_head == lane_head).astype(f32).astype(bf16)
    piece_head = lax.broadcasted_iota(jnp.int32, (HEAD_DIM, hq), 1) // lat

    def widen(compact):
        return jnp.concatenate([compact] * heads, axis=0) * diagonal[...]

    def score(keys, wide):
        scores = dot(keys, wide)
        top = jnp.max(scores, axis=0, keepdims=True)
        expo = jnp.exp(scores - top)
        return top, jnp.sum(expo, axis=0, keepdims=True), expo.astype(bf16)

    def weigh(weights, values):
        full = lax.dot_general(values, weights, (((0,), (0,)), ((), ())), preferred_element_type=f32)
        acc = full[0:HEAD_DIM]
        for h in range(1, heads):
            acc = jnp.where(piece_head == h, full[part(h, HEAD_DIM)], acc)
        return acc

    def latent_side(layer):
        lat_norm = (normalize(state[...]) * lgain[layer : layer + 1, :]).astype(bf16)
        query = dot(lat_norm, wq[layer]) * (HEAD_DIM ** (-0.5))
        return lat_norm, [rows_to_lanes(query[:, part(g, hd)].T, heads).astype(bf16) for g in range(GROUPS)]

    def self_block(layer, lat_norm, compact):
        kv = dot(lat_norm, wkv[layer]).astype(bf16)
        for g in range(GROUPS):
            top, total, weights = score(kv[:, part(2 * g, hd)], widen(compact[g]))
            self_st[g, 0:1, :] = top
            self_st[g, 1:2, :] = total
            self_acc[g] = weigh(weights, kv[:, part(2 * g + 1, hd)])

    for copy in loads[1:-1]:
        copy.wait()
    state[...] = latents[...]
    lat_norm, compact = latent_side(0)
    self_block(0, lat_norm, compact)
    for g in range(GROUPS):
        wide0[g] = widen(compact[g])

    row = lax.broadcasted_iota(jnp.int32, (frames, frames), 0)
    lane = lax.broadcasted_iota(jnp.int32, (frames, frames), 1)
    clip_col = jnp.zeros((frames, 1), jnp.int32)
    frame_row = lax.broadcasted_iota(jnp.int32, (frames, 1), 0)
    for f in range(frames):
        clip_col = jnp.where(frame_row == f, clip_s[f], clip_col)
    slot_col = clip_col - me + REACH
    seen = jnp.where((clip_col == clip_v[...]) & (lane < row), 1.0, 0.0)
    for step in range(1, BACK + 1):
        near(-step)(clip_copies[step - 1].wait_recv)
    for step in range(1, BACK + 1):
        seen += jnp.where(clip_col == near_clips[step - 1], 1.0, 0.0)
    index = jnp.sum(seen, axis=1, keepdims=True).astype(jnp.int32)
    times = table.shape[0]
    picker = (lax.broadcasted_iota(jnp.int32, (frames, times), 1) == index).astype(f32).astype(bf16)
    stamp = dot(picker, table[...])
    stamps[...] = stamp - jnp.mean(stamp, axis=-1, keepdims=True)

    def norm_frame(f, dst):
        stamp = stamps[pl.ds(f, 1), :]
        for r in range(patches // chunk):
            rows = part(r, chunk)
            value = centered[f, rows, :] + stamp
            scale = lax.rsqrt(jnp.mean(value * value, axis=-1, keepdims=True) + EPS)
            scales[f, rows, :] = jnp.broadcast_to(scale, (chunk, 128))
            dst[rows, :] = (value * scale * mgain[0:1, :]).astype(bf16)

    def norm_frame1(f, dst):
        stamp = stamps[pl.ds(f, 1), :]
        for r in range(patches // chunk):
            rows = part(r, chunk)
            value = centered[f, rows, :] + stamp
            scale = jnp.concatenate([scales[f, rows, :]] * (width // 128), axis=1)
            dst[rows, :] = (value * scale * mgain[1:2, :]).astype(bf16)

    def project(f, src, dst):
        kv = dot(src[...], wkv[0]).astype(bf16)
        dst[...] = kv[:, : 2 * hd]
        kv0[f] = kv[:, 2 * hd :]

    def project1(src, f):
        kv1[f] = dot(src[...], wkv[1]).astype(bf16)

    def score_frame(g, f, keys, wide, dst):
        tops[g, pl.ds(f, 1), :], totals[g, pl.ds(f, 1), :], dst[...] = score(keys, wide)

    even, odd = (norm_a, kv_a, p_a), (norm_b, kv_b, p_b)

    def stage_norm(f, buffers):
        norm_frame(f, buffers[0])

    def stage_project(f, buffers):
        project(f, buffers[0], buffers[1])

    def stage_score(f, buffers):
        score_frame(0, f, buffers[1][:, :hd], wide0[0], buffers[2])

    def stage_weigh(f, buffers):
        accs[0, f] = weigh(buffers[2][...], buffers[1][:, hd:])

    stage_norm(0, even)
    stage_norm(1, odd)
    stage_project(0, even)
    stage_norm(2, even)
    stage_score(0, even)
    stage_project(1, odd)
    stage_norm(3, odd)
    stage_weigh(0, even)
    stage_score(1, odd)
    stage_project(2, even)

    def pair(i, carry):
        f = 2 * i
        stage_norm(f, even)
        stage_weigh(f - 3, odd)
        stage_score(f - 2, even)
        stage_project(f - 1, odd)
        stage_norm(f + 1, odd)
        stage_weigh(f - 2, even)
        stage_score(f - 1, odd)
        stage_project(f, even)
        return carry

    lax.fori_loop(2, frames // 2, pair, 0)
    stage_weigh(frames - 3, odd)
    stage_score(frames - 2, even)
    stage_project(frames - 1, odd)
    stage_weigh(frames - 2, even)
    stage_score(frames - 1, odd)
    stage_weigh(frames - 1, odd)

    def attend(score_at, weigh_at):
        def four(i, carry):
            f = 4 * i
            score_at(f + 1, p_b)
            weigh_at(f, p_a)
            score_at(f + 2, p_a)
            weigh_at(f + 1, p_b)
            score_at(f + 3, p_b)
            weigh_at(f + 2, p_a)
            score_at(jnp.minimum(f + 4, frames - 1), p_a)
            weigh_at(f + 3, p_b)
            return carry

        score_at(0, p_a)
        lax.fori_loop(0, frames // 4, four, 0)

    def score0(f, dst):
        score_frame(1, f, kv0[f, :, :hd], wide0[1], dst)

    def weigh0(f, src):
        accs[1, f] = weigh(src[...], kv0[f, :, hd:])

    def gather_part(layer, g, slot):
        chosen = slot_col == slot
        top = jnp.max(jnp.where(chosen, tops[g], FLOOR), axis=0, keepdims=True)
        weight = jnp.where(chosen, jnp.exp(jnp.where(chosen, tops[g] - top, 0.0)), 0.0)
        acc = jnp.zeros((HEAD_DIM, hq), f32)
        for f in range(frames):
            acc += weight[f : f + 1, :] * accs[g, f]
        part_acc[layer, g, slot] = acc.astype(bf16)
        part_st[layer, slot, 2 * g : 2 * g + 1, :] = top
        part_st[layer, slot, 2 * g + 1 : 2 * g + 2, :] = jnp.sum(weight * totals[g], axis=0, keepdims=True)

    def part_copies(layer, g, slot):
        copies = [
            pltpu.make_async_remote_copy(
                src_ref=part_acc.at[layer, g, slot],
                dst_ref=got_acc.at[layer, g, slot],
                send_sem=acc_send.at[g, other(slot)],
                recv_sem=acc_recv.at[g, other(slot)],
                device_id=at(slot - REACH),
                device_id_type=MESH,
            )
        ]
        if g == GROUPS - 1:
            copies.append(
                pltpu.make_async_remote_copy(
                    src_ref=part_st.at[layer, slot],
                    dst_ref=got_st.at[layer, slot],
                    send_sem=st_send.at[other(slot)],
                    recv_sem=st_recv.at[other(slot)],
                    device_id=at(slot - REACH),
                    device_id_type=MESH,
                )
            )
        return copies

    def send_parts(layer, g):
        for slot in ORDER:
            gather_part(layer, g, slot)
            copies = part_copies(layer, g, slot)

            @near(slot - REACH)
            def _():
                for copy in copies:
                    copy.start()

        gather_part(layer, g, REACH)

    def wait_parts(layer):
        for g in range(GROUPS):
            for slot in ORDER:
                copies = part_copies(layer, g, slot)

                @near(REACH - slot)
                def _():
                    for copy in copies:
                        copy.wait_recv()

    def wait_sent(layer):
        for slot in ORDER:

            @near(slot - REACH)
            def _():
                for g in range(GROUPS):
                    for copy in part_copies(layer, g, slot):
                        copy.wait_send()

    def merge_parts(layer, g):
        sources = [(self_st[g, 0:1, :], self_st[g, 1:2, :], self_acc.at[g])]
        for held_st, held_acc, slots in ((part_st, part_acc, (REACH,)), (got_st, got_acc, ORDER)):
            for slot in slots:
                held = (
                    held_st[layer, slot, 2 * g : 2 * g + 1, :],
                    held_st[layer, slot, 2 * g + 1 : 2 * g + 2, :],
                )
                sources.append((*held, held_acc.at[layer, g, slot]))
        best = functools.reduce(jnp.maximum, [top for top, _, _ in sources])
        whole = jnp.zeros_like(best)
        combined = jnp.zeros((HEAD_DIM, hq), f32)
        for top, total, acc in sources:
            weight = jnp.exp(top - best)
            whole += weight * total
            combined += weight * acc[...].astype(f32)
        return rows_to_lanes((combined / whole).T, heads).astype(bf16)

    def attn_copy(layer, g):
        columns = pl.ds(pl.multiple_of(core * inner + g * hd, hd), hd)
        return columns, pltpu.make_async_remote_copy(
            src_ref=attn_all.at[layer, :, columns],
            dst_ref=attn_all.at[layer, :, columns],
            send_sem=at_send.at[layer, g],
            recv_sem=at_recv.at[layer, g],
            device_id=partner,
            device_id_type=MESH,
        )

    def share_attn(layer, g):
        columns, copy = attn_copy(layer, g)
        attn_all[layer, :, columns] = merge_parts(layer, g)
        copy.start()

    def update_state(layer):
        for g in range(GROUPS):
            attn_copy(layer, g)[1].wait_recv()
        state[...] += dot(attn_all[layer], wo[layer])

    def loop1(start, stop):
        def pair1(i, carry):
            f = 2 * i
            norm_frame1(f + 1, norm_b)
            project1(norm_a, f)
            norm_frame1(jnp.minimum(f + 2, frames - 1), norm_a)
            project1(norm_b, f + 1)
            return carry

        lax.fori_loop(start // 2, stop // 2, pair1, 0)

    send_parts(0, 0)

    attend(score0, weigh0)
    send_parts(0, 1)

    norm_frame1(0, norm_a)
    loop1(0, EARLY)
    loads[-1].wait()
    wo_copy.wait()
    wait_parts(0)
    share_attn(0, 0)
    share_attn(0, 1)
    update_state(0)

    lat_norm, compact = latent_side(1)

    def q_copy(g, slot):
        return pltpu.make_async_remote_copy(
            src_ref=q_near[g].at[REACH],
            dst_ref=q_near[g].at[SPAN - 1 - slot],
            send_sem=q_send.at[g, other(slot)],
            recv_sem=q_recv.at[g, other(SPAN - 1 - slot)],
            device_id=at(slot - REACH),
            device_id_type=MESH,
        )

    for g in range(GROUPS):
        q_near[g][REACH] = compact[g]
    for g in range(GROUPS):
        for slot in ORDER:
            near(slot - REACH)(q_copy(g, slot).start)
    self_block(1, lat_norm, compact)
    loop1(EARLY, frames)
    wait_sent(0)

    def score1(g, f, dst):
        slot = jnp.clip(clip_s[f] - me + REACH, 0, SPAN - 1)
        score_frame(g, f, kv1[f, :, part(2 * g, hd)], widen(q_near[g][slot]), dst)

    def weigh1(g, f, src):
        accs[g, f] = weigh(src[...], kv1[f, :, part(2 * g + 1, hd)])

    for g in range(GROUPS):
        for slot in ORDER:
            near(REACH - slot)(q_copy(g, slot).wait_recv)

        attend(functools.partial(score1, g), functools.partial(weigh1, g))
        send_parts(1, g)

    wait_parts(1)
    share_attn(1, 0)
    share_attn(1, 1)
    update_state(1)
    out_ref[...] = normalize(state[...]) * fgain[...]

    for step in range(1, BACK + 1):
        near(step)(clip_copies[step - 1].wait_send)
    for slot in ORDER:

        @near(slot - REACH)
        def _():
            for g in range(GROUPS):
                q_copy(g, slot).wait_send()

    wait_sent(1)
    for layer in range(LAYERS):
        for g in range(GROUPS):
            attn_copy(layer, g)[1].wait_send()


def local(n_dp, media, slot_clip, table, latents, mgain, lgain, fgain, wq, wk, wv, wo):
    frames, patches, width = media.shape
    layers, _, inner = wq.shape
    heads = inner // HEAD_DIM // GROUPS
    lat = latents.shape[0]
    hq = heads * lat
    hd = heads * HEAD_DIM
    vmem, dma = pltpu.VMEM, pltpu.SemaphoreType.DMA
    scratch = [
        vmem((1, frames), jnp.int32),
        vmem((BACK, 1, frames), jnp.int32),
        vmem((frames, patches, width), bf16),
        vmem(table.shape, bf16),
        vmem(latents.shape, f32),
        vmem(mgain.shape, f32),
        vmem(lgain.shape, f32),
        vmem((1, width), f32),
        vmem(wq.shape, bf16),
        vmem((layers, width, 2 * inner), bf16),
        vmem((layers, 2 * inner, width), bf16),
        vmem((frames, width), f32),
        vmem((patches, width), bf16),
        vmem((patches, width), bf16),
        vmem((frames, patches, 128), f32),
        vmem((frames, patches, width), f32),
        vmem((patches, 2 * hd), bf16),
        vmem((patches, 2 * hd), bf16),
        vmem((frames, patches, 2 * hd), bf16),
        vmem((patches, hq), bf16),
        vmem((patches, hq), bf16),
        vmem((frames, patches, 2 * inner), bf16),
        vmem((GROUPS, frames, HEAD_DIM, hq), f32),
        vmem((GROUPS, frames, hq), f32),
        vmem((GROUPS, frames, hq), f32),
        vmem((SPAN, HEAD_DIM, hq), bf16),
        vmem((SPAN, HEAD_DIM, hq), bf16),
        vmem((GROUPS, hd, hq), bf16),
        vmem((hd, hq), bf16),
        vmem((layers, GROUPS, SPAN, HEAD_DIM, hq), bf16),
        vmem((layers, SPAN, 2 * GROUPS, hq), f32),
        vmem((layers, GROUPS, SPAN, HEAD_DIM, hq), bf16),
        vmem((layers, SPAN, 2 * GROUPS, hq), f32),
        vmem((layers, lat, 2 * inner), bf16),
        vmem((GROUPS, HEAD_DIM, hq), f32),
        vmem((GROUPS, 2, hq), f32),
        vmem(latents.shape, f32),
        dma((8 + 2 * GROUPS,)),
        dma((frames // 4,)),
        dma((BACK,)),
        dma((BACK,)),
        dma(()),
        dma(()),
        dma((GROUPS, BACK)),
        dma((GROUPS, BACK)),
        dma((BACK,)),
        dma((BACK,)),
        dma((GROUPS, BACK)),
        dma((GROUPS, BACK)),
        dma((layers, GROUPS)),
        dma((layers, GROUPS)),
    ]
    result = pl.pallas_call(
        functools.partial(kernel, n_dp),
        out_shape=pltpu.VMEM(latents.shape, f32),
        in_specs=[pl.BlockSpec(memory_space=pltpu.SMEM)] + [pl.BlockSpec(memory_space=pltpu.HBM)] * 11,
        out_specs=pl.BlockSpec(memory_space=pltpu.VMEM),
        scratch_shapes=scratch,
        compiler_params=pltpu.CompilerParams(
            collective_id=0, has_side_effects=True, vmem_limit_bytes=56 * 1024 * 1024
        ),
        name="resample",
    )(slot_clip, slot_clip[None, :], media, table, latents, mgain, lgain, fgain[None, :], wq, wk, wv, wo)
    return result[None]


def solution(mesh):
    return jax.shard_map(
        functools.partial(local, mesh.shape["dp"]),
        mesh=mesh,
        in_specs=(
            P("dp", None, None),
            P("dp"),
            P(),
            P(),
            P(),
            P(),
            P(),
            P(None, None, "mp"),
            P(None, None, "mp"),
            P(None, None, "mp"),
            P(None, "mp", None),
        ),
        out_specs=P("dp", None, None),
        check_vma=False,
    )
```

time: 68.4 us -> 60.6 us (0.89)
  Pallas kernels: 66.6 us -> 59.8 us
  local copies, waits for them, and re-layouts: 1.67 us -> 0.71 us
    pallas_call x1, Pallas kernels: 66.6 us -> 59.8 us  [local(): pl.pallas_call(functools.partial(kernel, n_dp), out_shape=pltpu.VMEM(late...]
    unnamed x1, local copies, waits for them, and re-layouts: 1.67 us -> 0.71 us
where the time goes in v3:
time: 60.6 us; the launch traced here: 60.5 us
  Pallas kernels  59.8 us (99%)
  local copies, waits for them, and re-layouts  0.71 us (1%)
    pallas_call x1, Pallas kernels, local(): pl.pallas_call(functools.partial(kernel, n_dp), out_shape=pltpu.VMEM(late...  59.8 us

profile of v3, /device:TPU:25, one launch (start us, length us, event | category | flops | bytes accessed | tf_op | source)
XLA Modules:
  0.0 60.5 jit_solution(455701508649432715)
XLA Ops:
  0.0 59.8 %resample.1 = f32[64,1024]{1,0:T(8,128)S(1)} custom-call(s32[16]{0:T(128)} %clip_s.1, s32[1,16]{1,0:T(1,128)} %bitcast.5, bf16[16,256,1024]{2,1,0:T(8,128)(2,1)} %media_h.1, bf16[144,1024]{1,0:T(8,128)(2,1)} %table_h.1, f32[64,1024]{1,0:T(8,128)} %latents_h.1, f32[2,1024]{1,0:T(2,128)} %mgain_h.1, f32[2,1024]{1,0:T(2,128)} %lgain_h.1, f32[1,1024]{1,0:T(1,128)} %bitcast.4, ...), custom_call_target="tpu_custom_call" | custom-call | tf_op jit(solution)/shard_map/resample/pallas_call | solution.py:628
  59.8 0.7 %copy.13 = f32[1,64,1024]{2,1,0:T(8,128)} copy(f32[1,64,1024]{2,1,0:T(8,128)S(1)} %bitcast.3) | data formatting | bytes 524288

commit v4 on v3

--- a/solution.py
+++ b/solution.py
@@ -16,6 +16,9 @@
 EPS = 1e-05
 FLOOR = -1e30
 GROUPS = 2
+STEP = 4
+ATTEND = 16
+AHEAD = 2
 EARLY = 12
 ORDER = (0, 8, 1, 7, 2, 6, 3, 5)
 
@@ -78,11 +81,11 @@
     norm_b,
     scales,
     centered,
-    kv_a,
-    kv_b,
     kv0,
     p_a,
     p_b,
+    p_c,
+    p_d,
     kv1,
     accs,
     tops,
@@ -300,10 +303,8 @@
             scale = jnp.concatenate([scales[f, rows, :]] * (width // 128), axis=1)
             dst[rows, :] = (value * scale * mgain[1:2, :]).astype(bf16)
 
-    def project(f, src, dst):
-        kv = dot(src[...], wkv[0]).astype(bf16)
-        dst[...] = kv[:, : 2 * hd]
-        kv0[f] = kv[:, 2 * hd :]
+    def project0(src, f):
+        kv0[f] = dot(src[...], wkv[0]).astype(bf16)
 
     def project1(src, f):
         kv1[f] = dot(src[...], wkv[1]).astype(bf16)
@@ -311,72 +312,40 @@
     def score_frame(g, f, keys, wide, dst):
         tops[g, pl.ds(f, 1), :], totals[g, pl.ds(f, 1), :], dst[...] = score(keys, wide)
 
-    even, odd = (norm_a, kv_a, p_a), (norm_b, kv_b, p_b)
-
-    def stage_norm(f, buffers):
-        norm_frame(f, buffers[0])
-
-    def stage_project(f, buffers):
-        project(f, buffers[0], buffers[1])
-
-    def stage_score(f, buffers):
-        score_frame(0, f, buffers[1][:, :hd], wide0[0], buffers[2])
-
-    def stage_weigh(f, buffers):
-        accs[0, f] = weigh(buffers[2][...], buffers[1][:, hd:])
-
-    stage_norm(0, even)
-    stage_norm(1, odd)
-    stage_project(0, even)
-    stage_norm(2, even)
-    stage_score(0, even)
-    stage_project(1, odd)
-    stage_norm(3, odd)
-    stage_weigh(0, even)
-    stage_score(1, odd)
-    stage_project(2, even)
-
-    def pair(i, carry):
-        f = 2 * i
-        stage_norm(f, even)
-        stage_weigh(f - 3, odd)
-        stage_score(f - 2, even)
-        stage_project(f - 1, odd)
-        stage_norm(f + 1, odd)
-        stage_weigh(f - 2, even)
-        stage_score(f - 1, odd)
-        stage_project(f, even)
-        return carry
-
-    lax.fori_loop(2, frames // 2, pair, 0)
-    stage_weigh(frames - 3, odd)
-    stage_score(frames - 2, even)
-    stage_project(frames - 1, odd)
-    stage_weigh(frames - 2, even)
-    stage_score(frames - 1, odd)
-    stage_weigh(frames - 1, odd)
+    p_all = (p_a, p_b, p_c, p_d)
+
+    def norm_project(norm, project, start, stop, step):
+        def several(i, carry):
+            for j in range(step):
+                f = step * i + j
+                this, following = (norm_a, norm_b) if j % 2 == 0 else (norm_b, norm_a)
+                norm(jnp.minimum(f + 1, frames - 1) if j == step - 1 else f + 1, following)
+                project(this, f)
+            return carry
+
+        lax.fori_loop(start // step, stop // step, several, 0)
+
+    norm_frame(0, norm_a)
+    norm_project(norm_frame, project0, 0, frames, STEP)
 
     def attend(score_at, weigh_at):
-        def four(i, carry):
-            f = 4 * i
-            score_at(f + 1, p_b)
-            weigh_at(f, p_a)
-            score_at(f + 2, p_a)
-            weigh_at(f + 1, p_b)
-            score_at(f + 3, p_b)
-            weigh_at(f + 2, p_a)
-            score_at(jnp.minimum(f + 4, frames - 1), p_a)
-            weigh_at(f + 3, p_b)
+        def several(i, carry):
+            for j in range(ATTEND):
+                f = ATTEND * i + j
+                ahead = f + AHEAD
+                score_at(jnp.minimum(ahead, frames - 1) if j + AHEAD >= ATTEND else ahead, p_all[(j + AHEAD) % len(p_all)])
+                weigh_at(f, p_all[j % len(p_all)])
             return carry
 
-        score_at(0, p_a)
-        lax.fori_loop(0, frames // 4, four, 0)
-
-    def score0(f, dst):
-        score_frame(1, f, kv0[f, :, :hd], wide0[1], dst)
-
-    def weigh0(f, src):
-        accs[1, f] = weigh(src[...], kv0[f, :, hd:])
+        for j in range(AHEAD):
+            score_at(j, p_all[j])
+        lax.fori_loop(0, frames // ATTEND, several, 0)
+
+    def score0(g, f, dst):
+        score_frame(g, f, kv0[f, :, part(2 * g, hd)], wide0[g], dst)
+
+    def weigh0(g, f, src):
+        accs[g, f] = weigh(src[...], kv0[f, :, part(2 * g + 1, hd)])
 
     def gather_part(layer, g, slot):
         chosen = slot_col == slot
@@ -479,28 +448,18 @@
         copy.start()
 
     def update_state(layer):
+        theirs = pl.ds(pl.multiple_of((1 - core) * inner, inner), inner)
+        state[...] += dot(attn_all[layer, :, mine], wo[layer, mine, :])
         for g in range(GROUPS):
             attn_copy(layer, g)[1].wait_recv()
-        state[...] += dot(attn_all[layer], wo[layer])
-
-    def loop1(start, stop):
-        def pair1(i, carry):
-            f = 2 * i
-            norm_frame1(f + 1, norm_b)
-            project1(norm_a, f)
-            norm_frame1(jnp.minimum(f + 2, frames - 1), norm_a)
-            project1(norm_b, f + 1)
-            return carry
-
-        lax.fori_loop(start // 2, stop // 2, pair1, 0)
-
-    send_parts(0, 0)
-
-    attend(score0, weigh0)
-    send_parts(0, 1)
+        state[...] += dot(attn_all[layer, :, theirs], wo[layer, theirs, :])
+
+    for g in range(GROUPS):
+        attend(functools.partial(score0, g), functools.partial(weigh0, g))
+        send_parts(0, g)
 
     norm_frame1(0, norm_a)
-    loop1(0, EARLY)
+    norm_project(norm_frame1, project1, 0, EARLY, 2)
     loads[-1].wait()
     wo_copy.wait()
     wait_parts(0)
@@ -526,7 +485,7 @@
         for slot in ORDER:
             near(slot - REACH)(q_copy(g, slot).start)
     self_block(1, lat_norm, compact)
-    loop1(EARLY, frames)
+    norm_project(norm_frame1, project1, EARLY, frames, 2)
     wait_sent(0)
 
     def score1(g, f, dst):
@@ -589,9 +548,9 @@
         vmem((patches, width), bf16),
         vmem((frames, patches, 128), f32),
         vmem((frames, patches, width), f32),
-        vmem((patches, 2 * hd), bf16),
-        vmem((patches, 2 * hd), bf16),
-        vmem((frames, patches, 2 * hd), bf16),
+        vmem((frames, patches, 2 * inner), bf16),
+        vmem((patches, hq), bf16),
+        vmem((patches, hq), bf16),
         vmem((patches, hq), bf16),
         vmem((patches, hq), bf16),
         vmem((frames, patches, 2 * inner), bf16),

time: 60.6 us -> 57.6 us (0.950)
  Pallas kernels: 59.8 us -> 56.8 us
    pallas_call x1, Pallas kernels: 59.8 us -> 56.8 us  [local(): pl.pallas_call(functools.partial(kernel, n_dp), out_shape=pltpu.VMEM(late...]
where the time goes in v4:
time: 57.6 us; the launch traced here: 57.5 us
  Pallas kernels  56.8 us (99%)
  local copies, waits for them, and re-layouts  0.71 us (1%)
    pallas_call x1, Pallas kernels, local(): pl.pallas_call(functools.partial(kernel, n_dp), out_shape=pltpu.VMEM(late...  56.8 us

profile of v4, /device:TPU:25, one launch (start us, length us, event | category | flops | bytes accessed | tf_op | source)
XLA Modules:
  0.0 57.5 jit_solution(9624143101761859622)
XLA Ops:
  0.0 56.8 %resample.1 = f32[64,1024]{1,0:T(8,128)S(1)} custom-call(s32[16]{0:T(128)} %clip_s.1, s32[1,16]{1,0:T(1,128)} %bitcast.5, bf16[16,256,1024]{2,1,0:T(8,128)(2,1)} %media_h.1, bf16[144,1024]{1,0:T(8,128)(2,1)} %table_h.1, f32[64,1024]{1,0:T(8,128)} %latents_h.1, f32[2,1024]{1,0:T(2,128)} %mgain_h.1, f32[2,1024]{1,0:T(2,128)} %lgain_h.1, f32[1,1024]{1,0:T(1,128)} %bitcast.4, ...), custom_call_target="tpu_custom_call" | custom-call | tf_op jit(solution)/shard_map/resample/pallas_call | solution.py:587
  56.8 0.7 %copy.13 = f32[1,64,1024]{2,1,0:T(8,128)} copy(f32[1,64,1024]{2,1,0:T(8,128)S(1)} %bitcast.3) | data formatting | bytes 524288

commit v5 on v4

--- a/solution.py
+++ b/solution.py
@@ -16,7 +16,7 @@
 EPS = 1e-05
 FLOOR = -1e30
 GROUPS = 2
-STEP = 4
+STEP = 8
 ATTEND = 16
 AHEAD = 2
 EARLY = 12
@@ -52,7 +52,6 @@
 
 def kernel(
     n_dp,
-    clip_s,
     clip_h,
     media_h,
     table_h,
@@ -65,6 +64,7 @@
     wv_h,
     wo_h,
     out_ref,
+    clip_s,
     clip_v,
     near_clips,
     media,
@@ -110,9 +110,7 @@
     wo_recv,
     acc_send,
     acc_recv,
-    st_send,
     st_recv,
-    q_send,
     q_recv,
     at_send,
     at_recv,
@@ -157,6 +155,7 @@
     media_in = [media_copy(i) for i in range(frames // step4)]
     loads = [
         (clip_h, clip_v),
+        (clip_h, clip_s),
         (table_h, table),
         (latents_h, latents),
         (lgain_h, lgain),
@@ -170,7 +169,7 @@
         loads.append((wv_h.at[:, :, columns], wkv.at[:, :, pl.ds((2 * g + 1) * hd, hd)]))
     loads.append((wo_h, wo.at[:, mine, :]))
     loads = [pltpu.make_async_copy(a, b, local_sem.at[i]) for i, (a, b) in enumerate(loads)]
-    for copy in [loads[0]] + media_in + loads[1:]:
+    for copy in loads[:2] + media_in + loads[2:]:
         copy.start()
 
     loads[0].wait()
@@ -273,7 +272,7 @@
     clip_col = jnp.zeros((frames, 1), jnp.int32)
     frame_row = lax.broadcasted_iota(jnp.int32, (frames, 1), 0)
     for f in range(frames):
-        clip_col = jnp.where(frame_row == f, clip_s[f], clip_col)
+        clip_col = jnp.where(frame_row == f, clip_s[0, f], clip_col)
     slot_col = clip_col - me + REACH
     seen = jnp.where((clip_col == clip_v[...]) & (lane < row), 1.0, 0.0)
     for step in range(1, BACK + 1):
@@ -374,7 +373,7 @@
                 pltpu.make_async_remote_copy(
                     src_ref=part_st.at[layer, slot],
                     dst_ref=got_st.at[layer, slot],
-                    send_sem=st_send.at[other(slot)],
+                    send_sem=clip_send.at[other(slot)],
                     recv_sem=st_recv.at[other(slot)],
                     device_id=at(slot - REACH),
                     device_id_type=MESH,
@@ -454,6 +453,8 @@
             attn_copy(layer, g)[1].wait_recv()
         state[...] += dot(attn_all[layer, :, theirs], wo[layer, theirs, :])
 
+    for step in range(1, BACK + 1):
+        near(step)(clip_copies[step - 1].wait_send)
     for g in range(GROUPS):
         attend(functools.partial(score0, g), functools.partial(weigh0, g))
         send_parts(0, g)
@@ -473,7 +474,7 @@
         return pltpu.make_async_remote_copy(
             src_ref=q_near[g].at[REACH],
             dst_ref=q_near[g].at[SPAN - 1 - slot],
-            send_sem=q_send.at[g, other(slot)],
+            send_sem=acc_send.at[g, other(slot)],
             recv_sem=q_recv.at[g, other(SPAN - 1 - slot)],
             device_id=at(slot - REACH),
             device_id_type=MESH,
@@ -481,15 +482,15 @@
 
     for g in range(GROUPS):
         q_near[g][REACH] = compact[g]
+    wait_sent(0)
     for g in range(GROUPS):
         for slot in ORDER:
             near(slot - REACH)(q_copy(g, slot).start)
     self_block(1, lat_norm, compact)
     norm_project(norm_frame1, project1, EARLY, frames, 2)
-    wait_sent(0)
 
     def score1(g, f, dst):
-        slot = jnp.clip(clip_s[f] - me + REACH, 0, SPAN - 1)
+        slot = jnp.clip(clip_s[0, f] - me + REACH, 0, SPAN - 1)
         score_frame(g, f, kv1[f, :, part(2 * g, hd)], widen(q_near[g][slot]), dst)
 
     def weigh1(g, f, src):
@@ -500,6 +501,8 @@
             near(REACH - slot)(q_copy(g, slot).wait_recv)
 
         attend(functools.partial(score1, g), functools.partial(weigh1, g))
+        for slot in ORDER:
+            near(slot - REACH)(q_copy(g, slot).wait_send)
         send_parts(1, g)
 
     wait_parts(1)
@@ -507,15 +510,6 @@
     share_attn(1, 1)
     update_state(1)
     out_ref[...] = normalize(state[...]) * fgain[...]
-
-    for step in range(1, BACK + 1):
-        near(step)(clip_copies[step - 1].wait_send)
-    for slot in ORDER:
-
-        @near(slot - REACH)
-        def _():
-            for g in range(GROUPS):
-                q_copy(g, slot).wait_send()
 
     wait_sent(1)
     for layer in range(LAYERS):
@@ -532,6 +526,7 @@
     hd = heads * HEAD_DIM
     vmem, dma = pltpu.VMEM, pltpu.SemaphoreType.DMA
     scratch = [
+        pltpu.SMEM((1, frames), jnp.int32),
         vmem((1, frames), jnp.int32),
         vmem((BACK, 1, frames), jnp.int32),
         vmem((frames, patches, width), bf16),
@@ -569,7 +564,7 @@
         vmem((GROUPS, HEAD_DIM, hq), f32),
         vmem((GROUPS, 2, hq), f32),
         vmem(latents.shape, f32),
-        dma((8 + 2 * GROUPS,)),
+        dma((9 + 2 * GROUPS,)),
         dma((frames // 4,)),
         dma((BACK,)),
         dma((BACK,)),
@@ -578,8 +573,6 @@
         dma((GROUPS, BACK)),
         dma((GROUPS, BACK)),
         dma((BACK,)),
-        dma((BACK,)),
-        dma((GROUPS, BACK)),
         dma((GROUPS, BACK)),
         dma((layers, GROUPS)),
         dma((layers, GROUPS)),
@@ -587,14 +580,14 @@
     result = pl.pallas_call(
         functools.partial(kernel, n_dp),
         out_shape=pltpu.VMEM(latents.shape, f32),
-        in_specs=[pl.BlockSpec(memory_space=pltpu.SMEM)] + [pl.BlockSpec(memory_space=pltpu.HBM)] * 11,
+        in_specs=[pl.BlockSpec(memory_space=pltpu.HBM)] * 11,
         out_specs=pl.BlockSpec(memory_space=pltpu.VMEM),
         scratch_shapes=scratch,
         compiler_params=pltpu.CompilerParams(
             collective_id=0, has_side_effects=True, vmem_limit_bytes=56 * 1024 * 1024
         ),
         name="resample",
-    )(slot_clip, slot_clip[None, :], media, table, latents, mgain, lgain, fgain[None, :], wq, wk, wv, wo)
+    )(slot_clip[None, :], media, table, latents, mgain, lgain, fgain[None, :], wq, wk, wv, wo)
     return result[None]
 
 

time: 57.6 us -> 56.3 us (0.977)
  Pallas kernels: 56.8 us -> 55.5 us
    pallas_call x1, Pallas kernels: 56.8 us -> 55.5 us  [local(): pl.pallas_call(functools.partial(kernel, n_dp), out_shape=pltpu.VMEM(late...]
where the time goes in v5:
time: 56.3 us
  Pallas kernels  55.5 us (99%)
  local copies, waits for them, and re-layouts  0.71 us (1%)
    pallas_call x1, Pallas kernels, local(): pl.pallas_call(functools.partial(kernel, n_dp), out_shape=pltpu.VMEM(late...  55.5 us

profile of v5, /device:TPU:25, one launch (start us, length us, event | category | flops | bytes accessed | tf_op | source)
XLA Modules:
  0.0 56.3 jit_solution(9861527392523596772)
XLA Ops:
  0.0 55.5 %resample.1 = f32[64,1024]{1,0:T(8,128)S(1)} custom-call(s32[1,16]{1,0:T(1,128)} %bitcast.5, bf16[16,256,1024]{2,1,0:T(8,128)(2,1)} %media_h.1, bf16[144,1024]{1,0:T(8,128)(2,1)} %table_h.1, f32[64,1024]{1,0:T(8,128)} %latents_h.1, f32[2,1024]{1,0:T(2,128)} %mgain_h.1, f32[2,1024]{1,0:T(2,128)} %lgain_h.1, f32[1,1024]{1,0:T(1,128)} %bitcast.4, ...), custom_call_target="tpu_custom_call" | custom-call | tf_op jit(solution)/shard_map/resample/pallas_call | solution.py:580
  55.5 0.7 %copy.13 = f32[1,64,1024]{2,1,0:T(8,128)} copy(f32[1,64,1024]{2,1,0:T(8,128)S(1)} %bitcast.3) | data formatting | bytes 524288

commit v6 on v5

--- a/solution.py
+++ b/solution.py
@@ -137,7 +137,7 @@
     q_near = (q_near_a, q_near_b)
 
     barrier = pltpu.get_barrier_semaphore()
-    for step in (*range(-BACK, 0), *range(1, REACH + 1)):
+    for step in (-4, 4, -5, -3, 3, -6, -2, 2, -7, -1, 1, -8):
 
         @near(step)
         def _():
@@ -185,7 +185,7 @@
         )
         for step in range(1, BACK + 1)
     ]
-    for step in range(BACK, 0, -1):
+    for step in (4, 5, 3, 6, 2, 7, 1, 8):
         near(step)(clip_copies[step - 1].start)
     wo_copy = pltpu.make_async_remote_copy(
         src_ref=wo_h,
@@ -430,27 +430,24 @@
             combined += weight * acc[...].astype(f32)
         return rows_to_lanes((combined / whole).T, heads).astype(bf16)
 
-    def attn_copy(layer, g):
-        columns = pl.ds(pl.multiple_of(core * inner + g * hd, hd), hd)
-        return columns, pltpu.make_async_remote_copy(
-            src_ref=attn_all.at[layer, :, columns],
-            dst_ref=attn_all.at[layer, :, columns],
-            send_sem=at_send.at[layer, g],
-            recv_sem=at_recv.at[layer, g],
+    def attn_copy(layer):
+        return pltpu.make_async_remote_copy(
+            src_ref=attn_all.at[layer, :, mine],
+            dst_ref=attn_all.at[layer, :, mine],
+            send_sem=at_send.at[layer],
+            recv_sem=at_recv.at[layer],
             device_id=partner,
             device_id_type=MESH,
         )
 
-    def share_attn(layer, g):
-        columns, copy = attn_copy(layer, g)
-        attn_all[layer, :, columns] = merge_parts(layer, g)
-        copy.start()
+    def share_attn(layer):
+        attn_all[layer, :, mine] = jnp.concatenate([merge_parts(layer, g) for g in range(GROUPS)], axis=1)
+        attn_copy(layer).start()
 
     def update_state(layer):
         theirs = pl.ds(pl.multiple_of((1 - core) * inner, inner), inner)
         state[...] += dot(attn_all[layer, :, mine], wo[layer, mine, :])
-        for g in range(GROUPS):
-            attn_copy(layer, g)[1].wait_recv()
+        attn_copy(layer).wait_recv()
         state[...] += dot(attn_all[layer, :, theirs], wo[layer, theirs, :])
 
     for step in range(1, BACK + 1):
@@ -463,9 +460,9 @@
     norm_project(norm_frame1, project1, 0, EARLY, 2)
     loads[-1].wait()
     wo_copy.wait()
+    wait_sent(0)
     wait_parts(0)
-    share_attn(0, 0)
-    share_attn(0, 1)
+    share_attn(0)
     update_state(0)
 
     lat_norm, compact = latent_side(1)
@@ -482,7 +479,6 @@
 
     for g in range(GROUPS):
         q_near[g][REACH] = compact[g]
-    wait_sent(0)
     for g in range(GROUPS):
         for slot in ORDER:
             near(slot - REACH)(q_copy(g, slot).start)
@@ -498,23 +494,21 @@
 
     for g in range(GROUPS):
         for slot in ORDER:
+            near(slot - REACH)(q_copy(g, slot).wait_send)
+        for slot in ORDER:
             near(REACH - slot)(q_copy(g, slot).wait_recv)
 
         attend(functools.partial(score1, g), functools.partial(weigh1, g))
-        for slot in ORDER:
-            near(slot - REACH)(q_copy(g, slot).wait_send)
         send_parts(1, g)
 
     wait_parts(1)
-    share_attn(1, 0)
-    share_attn(1, 1)
+    share_attn(1)
     update_state(1)
     out_ref[...] = normalize(state[...]) * fgain[...]
 
     wait_sent(1)
     for layer in range(LAYERS):
-        for g in range(GROUPS):
-            attn_copy(layer, g)[1].wait_send()
+        attn_copy(layer).wait_send()
 
 
 def local(n_dp, media, slot_clip, table, latents, mgain, lgain, fgain, wq, wk, wv, wo):
@@ -574,8 +568,8 @@
         dma((GROUPS, BACK)),
         dma((BACK,)),
         dma((GROUPS, BACK)),
-        dma((layers, GROUPS)),
-        dma((layers, GROUPS)),
+        dma((layers,)),
+        dma((layers,)),
     ]
     result = pl.pallas_call(
         functools.partial(kernel, n_dp),

time: 56.3 us -> 55.7 us (0.989)
  Pallas kernels: 55.5 us -> 54.9 us
    pallas_call x1, Pallas kernels: 55.5 us -> 54.9 us  [local(): pl.pallas_call(functools.partial(kernel, n_dp), out_shape=pltpu.VMEM(late...]
where the time goes in v6:
time: 55.7 us
  Pallas kernels  54.9 us (99%)
  local copies, waits for them, and re-layouts  0.71 us (1%)
    pallas_call x1, Pallas kernels, local(): pl.pallas_call(functools.partial(kernel, n_dp), out_shape=pltpu.VMEM(late...  54.9 us

profile of v6, /device:TPU:25, one launch (start us, length us, event | category | flops | bytes accessed | tf_op | source)
XLA Modules:
  0.0 55.7 jit_solution(15980485224128160769)
XLA Ops:
  0.0 54.9 %resample.1 = f32[64,1024]{1,0:T(8,128)S(1)} custom-call(s32[1,16]{1,0:T(1,128)} %bitcast.5, bf16[16,256,1024]{2,1,0:T(8,128)(2,1)} %media_h.1, bf16[144,1024]{1,0:T(8,128)(2,1)} %table_h.1, f32[64,1024]{1,0:T(8,128)} %latents_h.1, f32[2,1024]{1,0:T(2,128)} %mgain_h.1, f32[2,1024]{1,0:T(2,128)} %lgain_h.1, f32[1,1024]{1,0:T(1,128)} %bitcast.4, ...), custom_call_target="tpu_custom_call" | custom-call | tf_op jit(solution)/shard_map/resample/pallas_call | solution.py:574
  54.9 0.7 %copy.13 = f32[1,64,1024]{2,1,0:T(8,128)} copy(f32[1,64,1024]{2,1,0:T(8,128)S(1)} %bitcast.3) | data formatting | bytes 524288

commit v7 on v6

--- a/solution.py
+++ b/solution.py
@@ -382,18 +382,21 @@
         return copies
 
     def send_parts(layer, g):
-        for slot in ORDER:
-            gather_part(layer, g, slot)
-            copies = part_copies(layer, g, slot)
-
-            @near(slot - REACH)
-            def _():
-                for copy in copies:
-                    copy.start()
-
-        gather_part(layer, g, REACH)
+        for first in range(0, len(ORDER), 2):
+            for slot in ORDER[first : first + 2]:
+                gather_part(layer, g, slot)
+            for slot in ORDER[first : first + 2]:
+                copies = part_copies(layer, g, slot)
+
+                @near(slot - REACH)
+                def _():
+                    for copy in copies:
+                        copy.start()
+
 
     def wait_parts(layer):
+        for g in range(GROUPS):
+            gather_part(layer, g, REACH)
         for g in range(GROUPS):
             for slot in ORDER:
                 copies = part_copies(layer, g, slot)

time: 55.7 us -> 55.5 us (level)
  no operation moved by 1% of the time
where the time goes in v7:
time: 55.5 us; the launch traced here: 55.4 us
  Pallas kernels  54.7 us (99%)
  local copies, waits for them, and re-layouts  0.71 us (1%)
    pallas_call x1, Pallas kernels, local(): pl.pallas_call(functools.partial(kernel, n_dp), out_shape=pltpu.VMEM(late...  54.7 us

profile of v7, /device:TPU:25, one launch (start us, length us, event | category | flops | bytes accessed | tf_op | source)
XLA Modules:
  0.0 55.4 jit_solution(2938747413762074737)
XLA Ops:
  0.0 54.7 %resample.1 = f32[64,1024]{1,0:T(8,128)S(1)} custom-call(s32[1,16]{1,0:T(1,128)} %bitcast.5, bf16[16,256,1024]{2,1,0:T(8,128)(2,1)} %media_h.1, bf16[144,1024]{1,0:T(8,128)(2,1)} %table_h.1, f32[64,1024]{1,0:T(8,128)} %latents_h.1, f32[2,1024]{1,0:T(2,128)} %mgain_h.1, f32[2,1024]{1,0:T(2,128)} %lgain_h.1, f32[1,1024]{1,0:T(1,128)} %bitcast.4, ...), custom_call_target="tpu_custom_call" | custom-call | tf_op jit(solution)/shard_map/resample/pallas_call | solution.py:577
  54.7 0.7 %copy.13 = f32[1,64,1024]{2,1,0:T(8,128)} copy(f32[1,64,1024]{2,1,0:T(8,128)S(1)} %bitcast.3) | data formatting | bytes 524288
